TPU v7x, 8 devices: a whole 2x2x1 slice. The times are simulated.
8 devices in a mesh: dp: 2 (over z, y), ep: 4 (over x, core).
Axes of the slice: x: 2, y: 2, z: 1, core: 2. Of those that a mesh axis runs over, the one named last changes fastest.
Arguments:
- tokens: bfloat16 [2048, 2048], P(('dp', 'ep')), parts along dimension 0
- expert_ids: int32 [2048, 2], P(('dp', 'ep')), parts along dimension 0
- gate_w: float32 [2048, 2], P(('dp', 'ep')), parts along dimension 0
- route_counts: int32 [8, 8], P(('dp', 'ep')), parts along dimension 0
- w_gate: bfloat16 [8, 2048, 5632], P('ep')
- w_up: bfloat16 [8, 2048, 5632], P('ep')
- w_down: bfloat16 [8, 5632, 2048], P('ep')
Outputs:
- output: bfloat16 [2048, 2048], P(('dp', 'ep')), parts along dimension 0
There are 2 independent parts. A program takes and returns all parts, laid end to end along the dimension named above; an argument that names none is the same for every part.
All inputs are finite; a program needn't handle non-finite values.
Results may differ from a plain program's by a relative error of at most 0.001.
Values are sent between devices in bfloat16 or wider.
A program may use at most 1 GiB of HBM per device.

v0:
```python
import jax
import jax.numpy as jnp
from jax import lax
from jax.sharding import PartitionSpec as P


def place_rows(expert_ids, counts_row, cap_rows, n_exp):
    tok_n, top_n = expert_ids.shape
    flat_ids = expert_ids.reshape(tok_n * top_n)
    onehot = (flat_ids[:, None] == jnp.arange(n_exp)[None, :]).astype(jnp.int32)
    before = jnp.cumsum(onehot, axis=0) - onehot
    slot_idx = jnp.sum(before * onehot, axis=1)
    row_limit = jnp.sum(onehot * counts_row[None, :], axis=1)
    buf_pos = jnp.where(slot_idx < row_limit, flat_ids * cap_rows + slot_idx, -1)
    return buf_pos.reshape(tok_n, top_n)


def expert_ffn(rows_in, w_gate, w_up, w_down):
    act_a = jnp.einsum("erd,edf->erf", rows_in, w_gate, preferred_element_type=jnp.float32)
    act_b = jnp.einsum("erd,edf->erf", rows_in, w_up, preferred_element_type=jnp.float32)
    hidden = (jax.nn.silu(act_a) * act_b).astype(jnp.bfloat16)
    return jnp.einsum("erf,efd->erd", hidden, w_down, preferred_element_type=jnp.float32).astype(jnp.bfloat16)


def solution(mesh):
    group_size = mesh.shape["ep"]
    row_spec = P(("dp", "ep"))

    def local_step(tokens, expert_ids, gate_w, route_counts, w_gate, w_up, w_down):
        tok_n = expert_ids.shape[0]
        n_local = w_gate.shape[0]
        model_dim = w_gate.shape[1]
        n_exp = n_local * group_size
        cap_rows = tok_n // 2
        buf_pos = place_rows(expert_ids, route_counts[0], cap_rows, n_exp)
        disp_mat = jnp.any(jnp.arange(n_exp * cap_rows)[:, None, None] == buf_pos[None, :, :], axis=2).astype(jnp.bfloat16)
        packed = jnp.dot(disp_mat, tokens, preferred_element_type=jnp.float32).astype(jnp.bfloat16)
        packed = packed.reshape(group_size, n_local, cap_rows, model_dim)
        arrived = lax.all_to_all(packed, "ep", 0, 2, tiled=True)
        expert_out = expert_ffn(arrived.reshape(n_local, group_size * cap_rows, model_dim), w_gate, w_up, w_down)
        returned = lax.all_to_all(expert_out.reshape(1, n_local, group_size * cap_rows, model_dim), "ep", 2, 0, tiled=True)
        picked = jnp.take(returned.reshape(n_exp * cap_rows, model_dim), jnp.maximum(buf_pos, 0), axis=0)
        weights = jnp.where(buf_pos >= 0, gate_w, 0.0)
        total_f32 = tokens.astype(jnp.float32) + jnp.sum(weights[:, :, None] * picked.astype(jnp.float32), axis=1)
        return total_f32.astype(jnp.bfloat16)

    return jax.shard_map(local_step, mesh=mesh, in_specs=(row_spec, row_spec, row_spec, row_spec, P("ep"), P("ep"), P("ep")), out_specs=row_spec, check_vma=False)
```

profile of v0, /device:TPU:0, one launch (start us, length us, event | category | flops | bytes accessed | tf_op | source)
XLA Modules:
  0.0 251.9 jit_solution(1691637732887453534)
XLA Ops:
  0.0 0.8 copy.43
  1.1 1.1 reduce-window.6
  2.3 0.2 slice_reduce_fusion
  2.5 0.8 select_reduce_fusion
  3.5 0.1 reduce_sum.34
  3.7 0.7 compare_select_fusion
  4.4 0.4 fusion.3
  4.8 2.5 convolution_convert_fusion
  7.3 52.5 %all_to_all.30 = bf16[4,2,128,2048]{3,2,1,0:T(8,128)(2,1)S(1)} all-to-all(bf16[4,2,128,2048]{3,2,1,0:T(8,128)(2,1)S(1)} %bitcast.37), channel_id=1, replica_groups=mesh['dp'=2,'ep'=4] {'ep'}, dimensions={0} | all-to-all | bytes 8388608 | tf_op jit(solution)/shard_map/all_to_all | solution.py:39
  59.9 0.5 copy.50
  60.4 2.1 copy-done
  62.5 31.7 %fusion.8 = f32[2,512,5632]{2,1,0:T(8,128)} fusion(bf16[2,512,2048]{2,1,0:T(8,128)(2,1)S(1)} %bitcast.39, bf16[2,2048,5632]{2,1,0:T(8,128)(2,1)} %param.11), kind=kOutput, calls=%fused_computation.25 | convolution fusion | flops 23622320128 | bytes 73400320 | tf_op jit(solution)/shard_map/erd,edf->erf/dot_general | solution.py:19
  94.2 36.4 %multiply_convert_fusion.6 = bf16[2,512,5632]{2,1,0:T(8,128)(2,1)} fusion(f32[2,512,5632]{2,1,0:T(8,128)} %fusion.8, bf16[2,512,2048]{2,1,0:T(8,128)(2,1)} %bitcast.40, bf16[2,2048,5632]{2,1,0:T(8,128)(2,1)} %param.12), kind=kOutput, calls=%fused_computation.1.clone.clone.clone.clone.1 | convolution fusion | flops 23656923136 | bytes 84934656 | tf_op jit(solution)/shard_map/erd,edf->erf/dot_general | solution.py:20
  130.5 33.0 %convert_bitcast_fusion = bf16[1,2,512,2048]{3,2,1,0:T(8,128)(2,1)} fusion(bf16[2,5632,2048]{2,1,0:T(8,128)(2,1)} %param.13, bf16[2,512,5632]{2,1,0:T(8,128)(2,1)} %multiply_convert_fusion.6), kind=kOutput, calls=%fused_computation.5 | convolution fusion | flops 23624417280 | bytes 61865984 | tf_op jit(solution)/shard_map/erf,efd->erd/dot_general | solution.py:22
  163.6 8.5 %copy.51 = bf16[1,2,512,2048]{3,1,0,2:T(2,128)(2,1)} copy(bf16[1,2,512,2048]{3,2,1,0:T(8,128)(2,1)} %convert_bitcast_fusion) | data formatting | bytes 8388608 | tf_op jit(solution)/shard_map/reshape | solution.py:41
  172.1 4.9 %all-to-all-start.1 = ((bf16[1,2,512,2048]{3,1,0,2:T(2,128)(2,1)}), bf16[1,2,512,2048]{3,1,0,2:T(2,128)(2,1)}, u32[]{:S(2)}, u32[]{:S(2)}) async-start(bf16[1,2,512,2048]{3,1,0,2:T(2,128)(2,1)} %copy.51), calls=%async_computation.1 | async-start | bytes 8388608 | tf_op jit(solution)/shard_map/all_to_all | solution.py:41
  177.1 0.1 reshape.59
  177.2 0.2 copy.49
  177.6 47.2 %all-to-all-done.1 = bf16[1,2,512,2048]{3,1,0,2:T(2,128)(2,1)} async-done(((bf16[1,2,512,2048]{3,1,0,2:T(2,128)(2,1)}), bf16[1,2,512,2048]{3,1,0,2:T(2,128)(2,1)}, u32[]{:S(2)}, u32[]{:S(2)}) %all-to-all-start.1) | async-done | bytes 4194336 | tf_op jit(solution)/shard_map/all_to_all | solution.py:41
  224.8 6.0 %copy.52 = bf16[1,2,4,128,2048]{4,3,1,2,0:T(8,128)(2,1)} copy(bf16[1,2,4,128,2048]{4,1,3,2,0:T(2,128)(2,1)} %bitcast.8) | data formatting | bytes 8388608 | tf_op jit(solution)/shard_map/all_to_all | solution.py:41
  230.8 7.1 %gather_fusion = bf16[512,2048]{1,0:T(8,128)(2,1)S(1)} fusion(bf16[1024,2048]{1,0:T(8,128)(2,1)} %bitcast.36, s32[1024]{0:T(1024)S(1)} %pad_clamp_fusion), kind=kCustom, calls=%fused_computation | custom fusion | bytes 4196352 | tf_op jit(solution)/shard_map/jit(_take)/gather | solution.py:42
  238.0 2.7 %reshape.58 = bf16[256,2,2048]{2,1,0:T(2,128)(2,1)} reshape(bf16[512,2048]{1,0:T(8,128)(2,1)S(1)} %gather_fusion) | data formatting | bytes 4194304 | tf_op jit(solution)/shard_map/jit(_take)/gather | solution.py:42
  240.7 9.9 %multiply_reduce_fusion = f32[256,2048]{1,0:T(8,128)S(1)} fusion(bf16[256,2,2048]{2,1,0:T(2,128)(2,1)} %reshape.58, pred[256,2]{1,0:T(8,128)(4,1)S(1)} %copy.49, f32[256,2]{1,0:T(8,128)S(1)} %copy.48), kind=kLoop, calls=%fused_computation.4 | loop fusion | flops 3670016 | bytes 4196864 | tf_op jit(solution)/shard_map/reduce_sum | solution.py:44
  250.6 1.3 add_convert_fusion
  (16 shorter events, 0.9 us)
Async XLA Ops:
  60.4 2.1 copy-start
  172.1 52.7 %all-to-all-start.1 = ((bf16[1,2,512,2048]{3,1,0,2:T(2,128)(2,1)}), bf16[1,2,512,2048]{3,1,0,2:T(2,128)(2,1)}, u32[]{:S(2)}, u32[]{:S(2)}) async-start(bf16[1,2,512,2048]{3,1,0,2:T(2,128)(2,1)} %copy.51), calls=%async_computation.1 | async-start | bytes 8388608 | tf_op jit(solution)/shard_map/all_to_all | solution.py:41
  238.0 12.6 %copy-start.1 = (bf16[256,2048]{1,0:T(8,128)(2,1)S(1)}, bf16[256,2048]{1,0:T(8,128)(2,1)}, u32[]{:S(2)}) copy-start(bf16[256,2048]{1,0:T(8,128)(2,1)} %param.7) | copy-start | bytes 3145732
where the time goes:
time: 252 us
  matrix products  104 us (41%)
  blocking collectives  52.5 us (21%)
  waiting for transfers between devices  47.2 us (19%)
  local copies, waits for them, and re-layouts  29.2 us (12%)
  other arithmetic  14.2 us (6%)
  starting transfers between devices  4.86 us (2%)
    all_to_all x1, blocking collectives, local_step(): arrived = lax.all_to_all(packed, 'ep', 0, 2, tiled=True)  52.5 us
    all_to_all x1, waiting for transfers between devices, local_step(): lax.all_to_all(expert_out.reshape(1, n_local, group_size * cap_rows, mode...  47.2 us
    dot_general x1, matrix products, expert_ffn(): jnp.einsum('erd,edf->erf', rows_in, w_up, preferred_element_type=jnp.floa...  36.4 us
    dot_general x1, matrix products, expert_ffn(): jnp.einsum('erf,efd->erd', hidden, w_down, preferred_element_type=jnp.flo...  33 us
    dot_general x1, matrix products, expert_ffn(): jnp.einsum('erd,edf->erf', rows_in, w_gate, preferred_element_type=jnp.fl...  31.7 us
    reduce_sum x1, other arithmetic, local_step(): jnp.sum(weights[:, :, None] * picked.astype(jnp.float32), axis=1)  9.9 us
    gather x2, local copies, waits for them, and re-layouts, local_step(): jnp.take(returned.reshape(n_exp * cap_rows, model_dim), jnp.maximum(buf_p...  9.8 us
    reshape x1, local copies, waits for them, and re-layouts, local_step(): expert_out.reshape(1, n_local, group_size * cap_rows, model_dim)  8.47 us
  transfers between devices with their start and end apart: 1, of which 1 were waited for; matrix products, arithmetic and copies ran while one was open for 0% of the time, Pallas kernels for 0%

commit v1 on v0

v1 whole, which is shorter than its diff:
```python
import functools

import jax
import jax.numpy as jnp
from jax import lax
from jax.experimental import pallas as pl
from jax.experimental.pallas import tpu as pltpu
from jax.sharding import PartitionSpec as P

N_CHUNKS = 4
N_COLS = 4
GU_SLOTS = 4
DN_SLOTS = 2
F_BLOCK = 512
BF = jnp.bfloat16
F32 = jnp.float32
PHASES = ((0, 0), (0, 2), (1, 2), (1, 0))


def kernel(
    tok_hbm, ids_ref, gate_ref, cnt_ref, wg_hbm, wu_hbm, wd_hbm, out_ref,
    tok, maps, comb, gates, rows_in, hid, acc, ysend, yrecv, gu, dn,
    s_own, s_gu, s_dn, xs_send, xs_recv, ps_send, ps_recv, rs_send, rs_recv, ms_send, ms_recv, ys_send, ys_recv,
):
    tok_n, dim = tok_hbm.shape
    cap = tok_n // 2
    ffn = wg_hbm.shape[2]
    n_gu = ffn // F_BLOCK
    n_phase = len(PHASES)
    chunk = tok_n // N_CHUNKS
    cw = dim // N_COLS

    me = lax.axis_index("ep")
    core = me % 2
    partner = me + 1 - 2 * core
    devs = (me, partner, (me + 2) % 4, (partner + 2) % 4)

    def remote(src, dst, send, recv, peer):
        return pltpu.make_async_remote_copy(
            src_ref=src, dst_ref=dst, send_sem=send, recv_sem=recv,
            device_id={"ep": devs[peer]}, device_id_type=pl.DeviceIdType.MESH,
        )

    def gu_copies(g):
        phase = g // n_gu
        cols = pl.ds(pl.multiple_of((g % n_gu) * F_BLOCK, F_BLOCK), F_BLOCK)
        slot = g % GU_SLOTS
        exp = phase // 2
        return (
            pltpu.make_async_copy(wg_hbm.at[exp, :, cols], gu.at[slot, 0], s_gu.at[slot, 0]),
            pltpu.make_async_copy(wu_hbm.at[exp, :, cols], gu.at[slot, 1], s_gu.at[slot, 1]),
        )

    def gu_start(g):
        for c in gu_copies(g):
            c.start()

    def dn_copy(d):
        exp = (d // N_COLS) // 2
        cols = pl.ds((d % N_COLS) * cw, cw)
        return pltpu.make_async_copy(wd_hbm.at[exp, :, cols], dn.at[d % DN_SLOTS], s_dn.at[d % DN_SLOTS])

    own_copy = pltpu.make_async_copy(tok_hbm, tok.at[0], s_own)
    own_copy.start()
    for g in range(GU_SLOTS - 1):
        gu_start(g)
    for d in range(DN_SLOTS):
        dn_copy(d).start()

    barrier = pltpu.get_barrier_semaphore()
    for peer in (1, 2, 3):
        pl.semaphore_signal(barrier, inc=1, device_id={"ep": devs[peer]}, device_id_type=pl.DeviceIdType.MESH)
    pl.semaphore_wait(barrier, 3)

    def rows_of(c):
        return pl.ds(c * chunk, chunk)

    x_copies = [remote(tok_hbm.at[rows_of(c)], tok.at[2, rows_of(c)], xs_send.at[c], xs_recv.at[c], 2) for c in range(N_CHUNKS)]
    r_copies = [remote(tok.at[2, rows_of(c)], tok.at[3, rows_of(c)], rs_send.at[c], rs_recv.at[c], 1) for c in range(N_CHUNKS)]
    p_copy = remote(tok_hbm, tok.at[1], ps_send, ps_recv, 1)
    x_copies[0].start()
    p_copy.start()
    for c in range(1, N_CHUNKS):
        x_copies[c].start()

    row = lax.broadcasted_iota(jnp.int32, (8, 1), 0)
    exp_row = row % 2 + 2 * jnp.where(row < 2, devs[0], jnp.where(row < 4, devs[1], jnp.where(row < 6, devs[2], devs[3])))
    hit0 = ids_ref[0:1, :] == exp_row
    hit1 = ids_ref[1:2, :] == exp_row
    hit = jnp.where(hit0 | hit1, 1.0, 0.0)
    earlier = jnp.where(
        lax.broadcasted_iota(jnp.int32, (tok_n, tok_n), 0) < lax.broadcasted_iota(jnp.int32, (tok_n, tok_n), 1), 1.0, 0.0
    ).astype(BF)
    slot = jnp.dot(hit.astype(BF), earlier, preferred_element_type=F32)
    limit = jnp.sum(jnp.where(exp_row == lax.broadcasted_iota(jnp.int32, (8, 8), 1), cnt_ref[...], 0), axis=1, keepdims=True)
    served = (hit > 0.0) & (slot < limit.astype(F32))
    slot1 = jnp.where(served, slot + 1.0, 0.0)
    maps[0] = slot1
    gate_rows = jnp.where(hit0, gate_ref[0:1, :], 0.0) + jnp.where(hit1, gate_ref[1:2, :], 0.0)
    gates[...] = jnp.where(served, gate_rows, 0.0).T
    slot1_t = slot1.T
    lane = lax.broadcasted_iota(jnp.int32, (tok_n, cap), 1).astype(F32) + 1.0
    for i in range(8):
        comb[i] = jnp.where(slot1_t[:, i : i + 1] == lane, 1.0, 0.0).astype(BF)
    m_copies = [remote(maps.at[0], maps.at[r], ms_send.at[r - 1], ms_recv.at[r - 1], r) for r in (1, 2, 3)]
    for c in m_copies:
        c.start()

    own_copy.wait()
    for k in range(N_COLS):
        cols = pl.ds(k * cw, cw)
        acc[:, cols] = tok[0, :, cols].astype(F32)

    def gather(phase):
        exp, first = PHASES[phase]
        for half in range(2):
            peer = first + half
            if peer > 0 and exp == 0:
                m_copies[peer - 1].wait_recv()
            if peer == 1 and exp == 0:
                p_copy.wait_recv()
            if peer == 3 and exp == 0:
                for c in r_copies:
                    c.wait_recv()
            slots = lax.broadcasted_iota(jnp.int32, (cap, tok_n), 0).astype(F32) + 1.0
            pick = jnp.where(maps[peer, 2 * peer + exp : 2 * peer + exp + 1, :] == slots, 1.0, 0.0).astype(BF)
            for k in range(N_COLS):
                cols = pl.ds(k * cw, cw)
                got = jnp.dot(pick, tok[peer, :, cols], preferred_element_type=F32)
                rows_in[half * cap : (half + 1) * cap, cols] = got.astype(BF)

    def relay(c):
        x_copies[c].wait_recv()
        r_copies[c].start()

    def gate_up(phase):
        def step(s, carry):
            g = phase * n_gu + s
            for c in gu_copies(g):
                c.wait()

            @pl.when(g + GU_SLOTS - 1 < n_phase * n_gu)
            def _():
                gu_start(g + GU_SLOTS - 1)

            sl = g % GU_SLOTS
            a = jnp.dot(rows_in[...], gu[sl, 0], preferred_element_type=F32)
            b = jnp.dot(rows_in[...], gu[sl, 1], preferred_element_type=F32)
            h = (a * jax.nn.sigmoid(a) * b).astype(BF)
            hid[:, pl.ds(pl.multiple_of(s * F_BLOCK, F_BLOCK), F_BLOCK)] = h

            if phase == 0:
                @pl.when(s == n_gu // 2)
                def _():
                    relay(0)
            return carry

        lax.fori_loop(0, n_gu, step, 0)

    def y_copy(phase, k, half):
        exp, first = PHASES[phase]
        peer = first + half
        return remote(ysend.at[exp, peer, k], yrecv.at[exp, peer, k], ys_send.at[exp, peer, k], ys_recv.at[exp, peer, k], peer)

    def fold(exp, peer, k):
        i = 2 * peer + exp
        cols = pl.ds(k * cw, cw)
        src = ysend if peer == 0 else yrecv
        picked = jnp.dot(comb[i], src[exp, peer, k], preferred_element_type=F32)
        acc[:, cols] += gates[:, i : i + 1] * picked

    def wait_y(exp, peer, k):
        phase = PHASES.index((exp, 0 if peer < 2 else 2))
        y_copy(phase, k, peer % 2).wait_recv()

    def down_step(phase, k):
        exp, first = PHASES[phase]
        d = phase * N_COLS + k
        dn_copy(d).wait()
        y = jnp.dot(hid[...], dn[d % DN_SLOTS], preferred_element_type=F32).astype(BF)
        ysend[exp, first, k] = y[:cap]
        ysend[exp, first + 1, k] = y[cap:]
        if d + DN_SLOTS < n_phase * N_COLS:
            dn_copy(d + DN_SLOTS).start()
        for half in range(2):
            if first + half > 0:
                y_copy(phase, k, half).start()

    def finish(k):
        for peer in (2, 3, 1):
            wait_y(1, peer, k)
            fold(1, peer, k)
        fold(1, 0, k)
        cols = pl.ds(k * cw, cw)
        out_ref[:, cols] = acc[:, cols].astype(BF)

    gather(0)
    gate_up(0)
    relay(1)
    for k in range(N_COLS):
        down_step(0, k)
        if k == N_COLS // 2 - 1:
            relay(2)
    relay(3)
    gather(1)
    gate_up(1)
    for k in range(N_COLS):
        down_step(1, k)
        wait_y(0, 1, k)
        fold(0, 1, k)
        fold(0, 0, k)
    gather(2)
    gate_up(2)
    for k in range(N_COLS):
        down_step(2, k)
    gather(3)
    gate_up(3)
    for k in range(N_COLS):
        for peer in (2, 3):
            wait_y(0, peer, k)
            fold(0, peer, k)
    for k in range(N_COLS):
        down_step(3, k)
        if k > 0:
            finish(k - 1)
    finish(N_COLS - 1)

    for c in x_copies + r_copies + m_copies + [p_copy]:
        c.wait_send()
    for phase, (exp, first) in enumerate(PHASES):
        for k in range(N_COLS):
            for half in range(2):
                if first + half > 0:
                    y_copy(phase, k, half).wait_send()


def solution(mesh):
    row_spec = P(("dp", "ep"))

    def local_step(tokens, expert_ids, gate_w, route_counts, w_gate, w_up, w_down):
        tok_n, dim = tokens.shape
        ffn = w_gate.shape[2]
        cap = tok_n // 2
        cw = dim // N_COLS
        vmem = pl.BlockSpec(memory_space=pltpu.VMEM)
        hbm = pl.BlockSpec(memory_space=pl.ANY)
        dma = pltpu.SemaphoreType.DMA
        return pl.pallas_call(
            kernel,
            name="moe",
            out_shape=jax.ShapeDtypeStruct((tok_n, dim), BF),
            in_specs=[hbm, vmem, vmem, vmem, hbm, hbm, hbm],
            out_specs=vmem,
            scratch_shapes=[
                pltpu.VMEM((4, tok_n, dim), BF),
                pltpu.VMEM((4, 8, tok_n), F32),
                pltpu.VMEM((8, tok_n, cap), BF),
                pltpu.VMEM((tok_n, 8), F32),
                pltpu.VMEM((2 * cap, dim), BF),
                pltpu.VMEM((2 * cap, ffn), BF),
                pltpu.VMEM((tok_n, dim), F32),
                pltpu.VMEM((2, 4, N_COLS, cap, cw), BF),
                pltpu.VMEM((2, 4, N_COLS, cap, cw), BF),
                pltpu.VMEM((GU_SLOTS, 2, dim, F_BLOCK), BF),
                pltpu.VMEM((DN_SLOTS, ffn, cw), BF),
                dma, dma((GU_SLOTS, 2)), dma((DN_SLOTS,)),
                dma((N_CHUNKS,)), dma((N_CHUNKS,)), dma, dma,
                dma((N_CHUNKS,)), dma((N_CHUNKS,)), dma((3,)), dma((3,)),
                dma((2, 4, N_COLS)), dma((2, 4, N_COLS)),
            ],
            compiler_params=pltpu.CompilerParams(
                collective_id=0, has_side_effects=True, vmem_limit_bytes=66_000_000
            ),
        )(tokens, expert_ids.T, gate_w.T, route_counts, w_gate, w_up, w_down)

    return jax.shard_map(local_step, mesh=mesh, in_specs=(row_spec, row_spec, row_spec, row_spec, P("ep"), P("ep"), P("ep")), out_specs=row_spec, check_vma=False)
```

time: 252 us -> 106 us (0.42)
  matrix products: 104 us -> 0 us
  Pallas kernels: 0 us -> 103 us
  blocking collectives: 52.5 us -> 0 us
  waiting for transfers between devices: 47.2 us -> 0 us
  local copies, waits for them, and re-layouts: 29.2 us -> 2.3 us
  other arithmetic: 14.2 us -> 0 us
  starting transfers between devices: 4.86 us -> 0 us
    dot_general x4 -> x0, matrix products: 104 us -> none  [the longest x1 36.4 us: expert_ffn(): jnp.einsum('erd,edf->erf', rows_in, w_up, preferred_element_type=jnp.floa...]
    pallas_call x0 -> x1, Pallas kernels: none -> 103 us  [local_step(): pl.pallas_call(kernel, name='moe', out_shape=jax.ShapeDtypeStruct((tok_n,...]
    all_to_all x1 -> x0, blocking collectives: 52.5 us -> none  [local_step(): arrived = lax.all_to_all(packed, 'ep', 0, 2, tiled=True)]
    all_to_all x1 -> x0, waiting for transfers between devices: 47.2 us -> none  [local_step(): lax.all_to_all(expert_out.reshape(1, n_local, group_size * cap_rows, mode...]
    reduce_sum x2 -> x0, other arithmetic: 10.7 us -> none  [the longest x1 9.9 us: local_step(): jnp.sum(weights[:, :, None] * picked.astype(jnp.float32), axis=1)]
    gather x2 -> x0, local copies, waits for them, and re-layouts: 9.8 us -> none  [local_step(): jnp.take(returned.reshape(n_exp * cap_rows, model_dim), jnp.maximum(buf_p...]
    reshape x1 -> x0, local copies, waits for them, and re-layouts: 8.47 us -> none  [local_step(): expert_out.reshape(1, n_local, group_size * cap_rows, model_dim)]
    all_to_all x2 -> x0, local copies, waits for them, and re-layouts: 6.55 us -> none  [the longest x1 6.03 us: local_step(): lax.all_to_all(expert_out.reshape(1, n_local, group_size * cap_rows, mode...]
  transfers between devices with their start and end apart: 1 -> 0, of which waited for: 1 -> 0; matrix products, arithmetic and copies ran while one was open for 0% -> 0% of each run, Pallas kernels for 0% -> 0%
where the time goes in v1:
time: 106 us
  Pallas kernels  103 us (97%)
  local copies, waits for them, and re-layouts  2.3 us (2%)
    pallas_call x1, Pallas kernels, local_step(): pl.pallas_call(kernel, name='moe', out_shape=jax.ShapeDtypeStruct((tok_n,...  103 us
    unnamed x1, local copies, waits for them, and re-layouts  2.3 us

profile of v1, /device:TPU:0, one launch (start us, length us, event | category | flops | bytes accessed | tf_op | source)
XLA Modules:
  0.0 105.8 jit_solution(5843231500895530992)
XLA Ops:
  0.0 103.4 %moe.1 = bf16[256,2048]{1,0:T(8,128)(2,1)} custom-call(bf16[256,2048]{1,0:T(8,128)(2,1)} %tok_hbm.1, s32[2,256]{1,0:T(2,128)} %bitcast.2, f32[2,256]{1,0:T(2,128)} %bitcast.3, s32[1,8]{1,0:T(1,128)} %cnt_ref.1, bf16[2,2048,5632]{2,1,0:T(8,128)(2,1)} %wg_hbm.1, bf16[2,2048,5632]{2,1,0:T(8,128)(2,1)} %wu_hbm.1, bf16[2,5632,2048]{2,1,0:T(8,128)(2,1)} %wd_hbm.1), custom_call_target="tpu_custom_call" | custom-call | tf_op jit(solution)/shard_map/moe/pallas_call | solution.py:248
  103.5 2.3 %copy.9 = bf16[256,2048]{1,0:T(8,128)(2,1)} copy(bf16[256,2048]{1,0:T(8,128)(2,1)} %moe.1) | data formatting | bytes 2097152

commit v2 on v1

--- a/solution.py
+++ b/solution.py
@@ -9,7 +9,8 @@
 
 N_CHUNKS = 4
 N_COLS = 4
-GU_SLOTS = 4
+GU_SLOTS = 8
+GU_AHEAD = 3
 DN_SLOTS = 2
 F_BLOCK = 512
 BF = jnp.bfloat16
@@ -41,31 +42,32 @@
             device_id={"ep": devs[peer]}, device_id_type=pl.DeviceIdType.MESH,
         )
 
-    def gu_copies(g):
-        phase = g // n_gu
-        cols = pl.ds(pl.multiple_of((g % n_gu) * F_BLOCK, F_BLOCK), F_BLOCK)
-        slot = g % GU_SLOTS
-        exp = phase // 2
+    def gu_slot(exp, blk):
+        return blk % GU_SLOTS if exp == 0 else (GU_SLOTS - 1 + n_gu * GU_SLOTS - blk) % GU_SLOTS
+
+    def gu_copies(exp, blk):
+        cols = pl.ds(pl.multiple_of(blk * F_BLOCK, F_BLOCK), F_BLOCK)
+        slot = gu_slot(exp, blk)
         return (
             pltpu.make_async_copy(wg_hbm.at[exp, :, cols], gu.at[slot, 0], s_gu.at[slot, 0]),
             pltpu.make_async_copy(wu_hbm.at[exp, :, cols], gu.at[slot, 1], s_gu.at[slot, 1]),
         )
 
-    def gu_start(g):
-        for c in gu_copies(g):
+    def gu_start(exp, blk):
+        for c in gu_copies(exp, blk):
             c.start()
 
-    def dn_copy(d):
-        exp = (d // N_COLS) // 2
-        cols = pl.ds((d % N_COLS) * cw, cw)
-        return pltpu.make_async_copy(wd_hbm.at[exp, :, cols], dn.at[d % DN_SLOTS], s_dn.at[d % DN_SLOTS])
+    def dn_slot(exp, blk):
+        return (blk + exp) % DN_SLOTS
+
+    def dn_copy(exp, blk):
+        slot = dn_slot(exp, blk)
+        return pltpu.make_async_copy(wd_hbm.at[exp, :, pl.ds(blk * cw, cw)], dn.at[slot], s_dn.at[slot])
 
     own_copy = pltpu.make_async_copy(tok_hbm, tok.at[0], s_own)
     own_copy.start()
-    for g in range(GU_SLOTS - 1):
-        gu_start(g)
-    for d in range(DN_SLOTS):
-        dn_copy(d).start()
+    for g in range(GU_AHEAD):
+        gu_start(0, g)
 
     barrier = pltpu.get_barrier_semaphore()
     for peer in (1, 2, 3):
@@ -134,39 +136,71 @@
         r_copies[c].start()
 
     def gate_up(phase):
+        exp = PHASES[phase][0]
+        n_held = n_gu - GU_SLOTS
+
         def step(s, carry):
-            g = phase * n_gu + s
-            for c in gu_copies(g):
-                c.wait()
-
-            @pl.when(g + GU_SLOTS - 1 < n_phase * n_gu)
-            def _():
-                gu_start(g + GU_SLOTS - 1)
-
-            sl = g % GU_SLOTS
+            if phase % 2 == 0:
+                blk = s
+                for c in gu_copies(exp, blk):
+                    c.wait()
+            else:
+                blk = n_gu - 1 - s
+
+                @pl.when(blk < n_held)
+                def _():
+                    for c in gu_copies(exp, blk):
+                        c.wait()
+
+            if phase == 0:
+                @pl.when(s + GU_AHEAD < n_gu)
+                def _():
+                    gu_start(0, s + GU_AHEAD)
+
+                for k in range(DN_SLOTS):
+                    @pl.when(s == n_gu - 5 + 2 * k)
+                    def _():
+                        dn_copy(0, k).start()
+
+                @pl.when(s == n_gu // 2)
+                def _():
+                    relay(0)
+            else:
+                if phase == 2:
+                    @pl.when((s >= 1) & (s + GU_SLOTS - 1 < n_gu))
+                    def _():
+                        gu_start(1, s + GU_SLOTS - 1)
+                else:
+                    @pl.when((s >= 1) & (s <= n_held))
+                    def _():
+                        gu_start(exp, n_held - s)
+
+                    if phase == 1:
+                        @pl.when(s > n_held)
+                        def _():
+                            gu_start(1, s - n_held - 1)
+
+            sl = gu_slot(exp, blk)
             a = jnp.dot(rows_in[...], gu[sl, 0], preferred_element_type=F32)
             b = jnp.dot(rows_in[...], gu[sl, 1], preferred_element_type=F32)
             h = (a * jax.nn.sigmoid(a) * b).astype(BF)
-            hid[:, pl.ds(pl.multiple_of(s * F_BLOCK, F_BLOCK), F_BLOCK)] = h
-
-            if phase == 0:
-                @pl.when(s == n_gu // 2)
-                def _():
-                    relay(0)
+            hid[:, pl.ds(pl.multiple_of(blk * F_BLOCK, F_BLOCK), F_BLOCK)] = h
             return carry
 
         lax.fori_loop(0, n_gu, step, 0)
+        if phase == 1:
+            gu_start(1, GU_SLOTS - 1)
 
     def y_copy(phase, k, half):
         exp, first = PHASES[phase]
         peer = first + half
-        return remote(ysend.at[exp, peer, k], yrecv.at[exp, peer, k], ys_send.at[exp, peer, k], ys_recv.at[exp, peer, k], peer)
+        return remote(ysend.at[exp, peer, k], yrecv.at[exp, peer - 1, k], ys_send.at[exp, peer, k], ys_recv.at[exp, peer, k], peer)
 
     def fold(exp, peer, k):
         i = 2 * peer + exp
         cols = pl.ds(k * cw, cw)
-        src = ysend if peer == 0 else yrecv
-        picked = jnp.dot(comb[i], src[exp, peer, k], preferred_element_type=F32)
+        rows = ysend[exp, 0, k] if peer == 0 else yrecv[exp, peer - 1, k]
+        picked = jnp.dot(comb[i], rows, preferred_element_type=F32)
         acc[:, cols] += gates[:, i : i + 1] * picked
 
     def wait_y(exp, peer, k):
@@ -175,13 +209,18 @@
 
     def down_step(phase, k):
         exp, first = PHASES[phase]
-        d = phase * N_COLS + k
-        dn_copy(d).wait()
-        y = jnp.dot(hid[...], dn[d % DN_SLOTS], preferred_element_type=F32).astype(BF)
+        step = k if phase % 2 == 0 else N_COLS - 1 - k
+        if phase % 2 == 0 or step >= DN_SLOTS:
+            dn_copy(exp, k).wait()
+        y = jnp.dot(hid[...], dn[dn_slot(exp, k)], preferred_element_type=F32).astype(BF)
         ysend[exp, first, k] = y[:cap]
         ysend[exp, first + 1, k] = y[cap:]
-        if d + DN_SLOTS < n_phase * N_COLS:
-            dn_copy(d + DN_SLOTS).start()
+        if phase % 2 == 0 and step + DN_SLOTS < N_COLS:
+            dn_copy(exp, k + DN_SLOTS).start()
+        if phase % 2 == 1 and step < N_COLS - DN_SLOTS:
+            dn_copy(exp, N_COLS - DN_SLOTS - 1 - step).start()
+        if phase == 1 and step >= N_COLS - DN_SLOTS:
+            dn_copy(1, step - (N_COLS - DN_SLOTS)).start()
         for half in range(2):
             if first + half > 0:
                 y_copy(phase, k, half).start()
@@ -204,7 +243,7 @@
     relay(3)
     gather(1)
     gate_up(1)
-    for k in range(N_COLS):
+    for k in reversed(range(N_COLS)):
         down_step(1, k)
         wait_y(0, 1, k)
         fold(0, 1, k)
@@ -219,11 +258,11 @@
         for peer in (2, 3):
             wait_y(0, peer, k)
             fold(0, peer, k)
-    for k in range(N_COLS):
+    for k in reversed(range(N_COLS)):
         down_step(3, k)
-        if k > 0:
-            finish(k - 1)
-    finish(N_COLS - 1)
+        if k < N_COLS - 1:
+            finish(k + 1)
+    finish(0)
 
     for c in x_copies + r_copies + m_copies + [p_copy]:
         c.wait_send()
@@ -260,7 +299,7 @@
                 pltpu.VMEM((2 * cap, ffn), BF),
                 pltpu.VMEM((tok_n, dim), F32),
                 pltpu.VMEM((2, 4, N_COLS, cap, cw), BF),
-                pltpu.VMEM((2, 4, N_COLS, cap, cw), BF),
+                pltpu.VMEM((2, 3, N_COLS, cap, cw), BF),
                 pltpu.VMEM((GU_SLOTS, 2, dim, F_BLOCK), BF),
                 pltpu.VMEM((DN_SLOTS, ffn, cw), BF),
                 dma, dma((GU_SLOTS, 2)), dma((DN_SLOTS,)),
@@ -269,7 +308,7 @@
                 dma((2, 4, N_COLS)), dma((2, 4, N_COLS)),
             ],
             compiler_params=pltpu.CompilerParams(
-                collective_id=0, has_side_effects=True, vmem_limit_bytes=66_000_000
+                collective_id=0, has_side_effects=True, vmem_limit_bytes=67_000_000
             ),
         )(tokens, expert_ids.T, gate_w.T, route_counts, w_gate, w_up, w_down)
 

time: 106 us -> 105 us (level)
  no operation moved by 1% of the time
where the time goes in v2:
time: 105 us
  Pallas kernels  103 us (98%)
  local copies, waits for them, and re-layouts  2.3 us (2%)
    pallas_call x1, Pallas kernels, local_step(): pl.pallas_call(kernel, name='moe', out_shape=jax.ShapeDtypeStruct((tok_n,...  103 us
    unnamed x1, local copies, waits for them, and re-layouts  2.3 us

profile of v2, /device:TPU:0, one launch (start us, length us, event | category | flops | bytes accessed | tf_op | source)
XLA Modules:
  0.0 104.9 jit_solution(749489502680852953)
XLA Ops:
  0.0 102.6 %moe.1 = bf16[256,2048]{1,0:T(8,128)(2,1)} custom-call(bf16[256,2048]{1,0:T(8,128)(2,1)} %tok_hbm.1, s32[2,256]{1,0:T(2,128)} %bitcast.2, f32[2,256]{1,0:T(2,128)} %bitcast.3, s32[1,8]{1,0:T(1,128)} %cnt_ref.1, bf16[2,2048,5632]{2,1,0:T(8,128)(2,1)} %wg_hbm.1, bf16[2,2048,5632]{2,1,0:T(8,128)(2,1)} %wu_hbm.1, bf16[2,5632,2048]{2,1,0:T(8,128)(2,1)} %wd_hbm.1), custom_call_target="tpu_custom_call" | custom-call | tf_op jit(solution)/shard_map/moe/pallas_call | solution.py:287
  102.6 2.3 %copy.9 = bf16[256,2048]{1,0:T(8,128)(2,1)} copy(bf16[256,2048]{1,0:T(8,128)(2,1)} %moe.1) | data formatting | bytes 2097152

commit v3 on v0

v3 whole, which is shorter than its diff:
```python
import jax
import jax.numpy as jnp
from jax import lax
from jax.experimental import pallas as pl
from jax.experimental.pallas import tpu as pltpu
from jax.sharding import PartitionSpec as P

N_CHUNKS = 4
N_COLS = 4
GU_SLOTS = 8
DN_SLOTS = 2
F_BLOCK = 512
GROUPS = ((0, 4), (4, 8), (8, 11))
BF = jnp.bfloat16
F32 = jnp.float32
N_PHASE = 4
FOLDS = ((1, 0), (0, 0), (0, 1), (1, 1))
SENT = 8
ZERO = 14


def kernel(
    tok_hbm, ids_ref, gate_ref, cnt_ref, wg_hbm, wu_hbm, wd_hbm, out_hbm,
    tok, maps, comb, gates, rows_in, hid, acc, ybuf, gu, dn,
    s_own, s_gu, s_dn, xs_send, xs_recv, ps_send, ps_recv, rs_send, rs_recv, ms_send, ms_recv, ys_send, ys_recv, s_out,
):
    tok_n, dim = tok_hbm.shape
    cap = tok_n // 2
    ffn = wg_hbm.shape[2]
    n_gu = ffn // F_BLOCK
    chunk = tok_n // N_CHUNKS
    cw = dim // N_COLS

    me = lax.axis_index("ep")
    partner = me + 1 - 2 * (me % 2)
    across = (me + 2) % 4
    diagonal = (partner + 2) % 4
    devs = (me, partner, across, diagonal)

    def remote(src, dst, send, recv, dev):
        return pltpu.make_async_remote_copy(
            src_ref=src, dst_ref=dst, send_sem=send, recv_sem=recv,
            device_id={"ep": dev}, device_id_type=pl.DeviceIdType.MESH,
        )

    def gu_slot(exp, blk):
        return jnp.where(exp == 0, blk % GU_SLOTS, (GU_SLOTS - 1 + n_gu * GU_SLOTS - blk) % GU_SLOTS)

    def gu_copies(exp, blk):
        cols = pl.ds(pl.multiple_of(blk * F_BLOCK, F_BLOCK), F_BLOCK)
        slot = gu_slot(exp, blk)
        return (
            pltpu.make_async_copy(wg_hbm.at[exp, :, cols], gu.at[slot, 0], s_gu.at[slot, 0]),
            pltpu.make_async_copy(wu_hbm.at[exp, :, cols], gu.at[slot, 1], s_gu.at[slot, 1]),
        )

    def gu_start(exp, blks):
        for blk in blks:
            for c in gu_copies(exp, blk):
                c.start()

    def dn_copy(d):
        cols = pl.ds(pl.multiple_of((d % N_COLS) * cw, cw), cw)
        slot = d % DN_SLOTS
        return pltpu.make_async_copy(wd_hbm.at[d // N_COLS // 2, :, cols], dn.at[slot], s_dn.at[slot])

    own_copy = pltpu.make_async_copy(tok_hbm, tok.at[0], s_own)
    own_copy.start()
    gu_start(0, range(4))

    barrier = pltpu.get_barrier_semaphore()
    for peer in (1, 2, 3):
        pl.semaphore_signal(barrier, inc=1, device_id={"ep": devs[peer]}, device_id_type=pl.DeviceIdType.MESH)
    pl.semaphore_wait(barrier, 3)

    def rows_of(c):
        return pl.ds(c * chunk, chunk)

    x_copies = [remote(tok_hbm.at[rows_of(c)], tok.at[2, rows_of(c)], xs_send.at[c], xs_recv.at[c], across) for c in range(N_CHUNKS)]
    r_copies = [remote(tok.at[2, rows_of(c)], tok.at[3, rows_of(c)], rs_send.at[c], rs_recv.at[c], partner) for c in range(N_CHUNKS)]
    p_copy = remote(tok_hbm, tok.at[1], ps_send, ps_recv, partner)
    x_copies[0].start()
    p_copy.start()
    for c in range(1, N_CHUNKS):
        x_copies[c].start()

    row = lax.broadcasted_iota(jnp.int32, (8, 1), 0)
    exp_row = row % 2 + 2 * jnp.where(row < 2, devs[0], jnp.where(row < 4, devs[1], jnp.where(row < 6, devs[2], devs[3])))
    hit0 = ids_ref[0:1, :] == exp_row
    hit1 = ids_ref[1:2, :] == exp_row
    hit = jnp.where(hit0 | hit1, 1.0, 0.0)
    earlier = jnp.where(
        lax.broadcasted_iota(jnp.int32, (tok_n, tok_n), 0) < lax.broadcasted_iota(jnp.int32, (tok_n, tok_n), 1), 1.0, 0.0
    ).astype(BF)
    slot = jnp.dot(hit.astype(BF), earlier, preferred_element_type=F32)
    limit = jnp.sum(jnp.where(exp_row == lax.broadcasted_iota(jnp.int32, (8, 8), 1), cnt_ref[...], 0), axis=1, keepdims=True)
    served = (hit > 0.0) & (slot < limit.astype(F32))
    slot1 = jnp.where(served, slot + 1.0, 0.0)
    maps[0] = slot1
    m_copies = [remote(maps.at[0], maps.at[r], ms_send.at[r - 1], ms_recv.at[r - 1], devs[r]) for r in (1, 2, 3)]
    for c in m_copies:
        c.start()
    gates_t = (jnp.where(hit0, gate_ref[0:1, :], 0.0) + jnp.where(hit1, gate_ref[1:2, :], 0.0)).T
    slot1_t = slot1.T
    lane = lax.broadcasted_iota(jnp.int32, (tok_n, cap), 1).astype(F32) + 1.0
    for f, (exp, side) in enumerate(FOLDS):
        for half in range(2):
            i = 2 * (2 * side + half) + exp
            comb[f, half] = jnp.where(slot1_t[:, i : i + 1] == lane, 1.0, 0.0).astype(BF)
            gates[f, :, half : half + 1] = gates_t[:, i : i + 1]
    for k in range(N_COLS):
        ybuf[ZERO, k] = jnp.zeros((cap, cw), BF)

    own_copy.wait()
    for k in range(N_COLS):
        cols = pl.ds(k * cw, cw)
        acc[:, cols] = tok[0, :, cols].astype(F32)

    def relay(c):
        x_copies[c].wait_recv()
        r_copies[c].start()

    def y_copy(exp, peer, k, dev):
        return remote(
            ybuf.at[SENT + 3 * exp + peer - 1, k], ybuf.at[4 * exp + peer, k], ys_send.at[exp, peer, k], ys_recv.at[exp, peer, k], dev
        )

    def folded(f, srcs, k):
        total = acc[:, k * cw : (k + 1) * cw]
        for half in range(2):
            picked = jnp.dot(comb[f, half], ybuf[srcs[half], k], preferred_element_type=F32)
            total += gates[f, :, half : half + 1] * picked
        return total

    def phase_step(p, carry):
        exp = p // 2
        rev = p % 2
        side = ((p + 1) // 2) % 2
        base = jnp.where(side == 0, me, across)
        base_partner = jnp.where(side == 0, partner, diagonal)

        @pl.when(p == 0)
        def _():
            p_copy.wait_recv()
            m_copies[0].wait_recv()

        @pl.when(p == 1)
        def _():
            relay(N_CHUNKS - 1)
            m_copies[1].wait_recv()
            m_copies[2].wait_recv()
            for c in r_copies:
                c.wait_recv()

        @pl.when(p > 0)
        def _():
            dn_copy(p * N_COLS + 1).start()

        def blk_of(s):
            return s + rev * (n_gu - 1 - 2 * s)

        for n, (first, last) in enumerate(GROUPS):
            @pl.when((rev == 0) | (n == 2))
            def _():
                for s in range(first, last):
                    for c in gu_copies(exp, blk_of(s)):
                        c.wait()

            @pl.when(p == 0)
            def _():
                if n == 0:
                    gu_start(0, range(4, 8))
                elif n == 1:
                    gu_start(0, range(8, n_gu))
                    dn_copy(0).start()
                else:
                    dn_copy(1).start()
                    relay(0)

            if n == 1:
                @pl.when(p == 1)
                def _():
                    gu_start(0, (2, 1, 0))
                    gu_start(1, (0,))

                @pl.when(p == 2)
                def _():
                    gu_start(1, (8, 9, 10))

                @pl.when(p == 3)
                def _():
                    gu_start(1, (2, 1, 0))
            elif n == 2:
                @pl.when(p == 1)
                def _():
                    gu_start(1, (1, 2, 3, 4))

            if n == 0:
                for half in range(2):
                    peer = 2 * side + half
                    slots = lax.broadcasted_iota(jnp.int32, (cap, tok_n), 0).astype(F32) + 1.0
                    pick = jnp.where(maps[peer, pl.ds(2 * peer + exp, 1), :] == slots, 1.0, 0.0).astype(BF)
                    for k in range(N_COLS):
                        cols = slice(k * cw, (k + 1) * cw)
                        got = jnp.dot(pick, tok[peer, :, cols], preferred_element_type=F32)
                        rows_in[half * cap : (half + 1) * cap, cols] = got.astype(BF)

            for s in range(first, last):
                sl = gu_slot(exp, blk_of(s))
                a = jnp.dot(rows_in[...], gu[sl, 0], preferred_element_type=F32)
                b = jnp.dot(rows_in[...], gu[sl, 1], preferred_element_type=F32)
                hid[:, pl.ds(pl.multiple_of(blk_of(s) * F_BLOCK, F_BLOCK), F_BLOCK)] = (a * jax.nn.sigmoid(a) * b).astype(BF)

        f_exp = p // 3
        f_side = p // 2
        srcs = [jnp.where(p == 0, ZERO, 4 * f_exp + 2 * f_side + half) for half in range(2)]
        top = jnp.where(side == 0, 4 * exp, SENT + 3 * exp + 1)
        low = SENT + 3 * exp + 2 * side
        for k in range(N_COLS):
            d = p * N_COLS + k
            dn_copy(d).wait()

            @pl.when(p > 0)
            def _():
                y_copy(f_exp, 2 * f_side + 1, k, me).wait_recv()

            @pl.when(p > 1)
            def _():
                y_copy(f_exp, 2, k, me).wait_recv()

            if k > 0:
                @pl.when(d + 1 < N_PHASE * N_COLS)
                def _():
                    dn_copy(d + 1).start()
            else:
                @pl.when(p == 1)
                def _():
                    gu_start(1, (5, 6, 7))

            if k % 2 == 0:
                @pl.when(p == 0)
                def _():
                    relay(1 + k // 2)

            acc[:, k * cw : (k + 1) * cw] = folded(p, srcs, k)
            y = jnp.dot(hid[...], dn[d % DN_SLOTS], preferred_element_type=F32).astype(BF)
            ybuf[top, k] = y[:cap]
            ybuf[low, k] = y[cap:]
            y_copy(exp, 2 * side + 1, k, base_partner).start()

            @pl.when(side == 1)
            def _():
                y_copy(exp, 2, k, base).start()
        return carry

    lax.fori_loop(0, N_PHASE, phase_step, 0)

    outs = []
    for k in range(N_COLS):
        y_copy(1, 1, k, partner).wait_recv()
        cols = slice(k * cw, (k + 1) * cw)
        rows_in[:, cols] = folded(0, (4, 5), k).astype(BF)
        outs.append(pltpu.make_async_copy(rows_in.at[:, cols], out_hbm.at[:, cols], s_out.at[k]))
        outs[k].start()

    for c in x_copies + r_copies + m_copies + [p_copy]:
        c.wait_send()
    for exp in range(2):
        for peer in range(1, 4):
            for k in range(N_COLS):
                y_copy(exp, peer, k, devs[peer]).wait_send()
    for c in outs:
        c.wait()


def solution(mesh):
    row_spec = P(("dp", "ep"))

    def local_step(tokens, expert_ids, gate_w, route_counts, w_gate, w_up, w_down):
        tok_n, dim = tokens.shape
        ffn = w_gate.shape[2]
        cap = tok_n // 2
        cw = dim // N_COLS
        vmem = pl.BlockSpec(memory_space=pltpu.VMEM)
        hbm = pl.BlockSpec(memory_space=pl.ANY)
        dma = pltpu.SemaphoreType.DMA
        return pl.pallas_call(
            kernel,
            name="moe",
            out_shape=jax.ShapeDtypeStruct((tok_n, dim), BF),
            in_specs=[hbm, vmem, vmem, vmem, hbm, hbm, hbm],
            out_specs=hbm,
            scratch_shapes=[
                pltpu.VMEM((4, tok_n, dim), BF),
                pltpu.VMEM((4, 8, tok_n), F32),
                pltpu.VMEM((4, 2, tok_n, cap), BF),
                pltpu.VMEM((4, tok_n, 2), F32),
                pltpu.VMEM((2 * cap, dim), BF),
                pltpu.VMEM((2 * cap, ffn), BF),
                pltpu.VMEM((tok_n, dim), F32),
                pltpu.VMEM((ZERO + 1, N_COLS, cap, cw), BF),
                pltpu.VMEM((GU_SLOTS, 2, dim, F_BLOCK), BF),
                pltpu.VMEM((DN_SLOTS, ffn, cw), BF),
                dma, dma((GU_SLOTS, 2)), dma((DN_SLOTS,)),
                dma((N_CHUNKS,)), dma((N_CHUNKS,)), dma, dma,
                dma((N_CHUNKS,)), dma((N_CHUNKS,)), dma((3,)), dma((3,)),
                dma((2, 4, N_COLS)), dma((2, 4, N_COLS)), dma((N_COLS,)),
            ],
            compiler_params=pltpu.CompilerParams(
                collective_id=0, has_side_effects=True, vmem_limit_bytes=67_000_000
            ),
        )(tokens, expert_ids.T, gate_w.T, route_counts, w_gate, w_up, w_down)

    return jax.shard_map(local_step, mesh=mesh, in_specs=(row_spec, row_spec, row_spec, row_spec, P("ep"), P("ep"), P("ep")), out_specs=row_spec, check_vma=False)
```

time: 252 us -> 108 us (0.43)
  Pallas kernels: 0 us -> 105 us
  matrix products: 104 us -> 0 us
  blocking collectives: 52.5 us -> 0 us
  waiting for transfers between devices: 47.2 us -> 0 us
  local copies, waits for them, and re-layouts: 29.2 us -> 2.3 us
  other arithmetic: 14.2 us -> 0 us
  starting transfers between devices: 4.86 us -> 0 us
    pallas_call x0 -> x1, Pallas kernels: none -> 105 us  [local_step(): pl.pallas_call(kernel, name='moe', out_shape=jax.ShapeDtypeStruct((tok_n,...]
    dot_general x4 -> x0, matrix products: 104 us -> none  [the longest x1 36.4 us: expert_ffn(): jnp.einsum('erd,edf->erf', rows_in, w_up, preferred_element_type=jnp.floa...]
    all_to_all x1 -> x0, blocking collectives: 52.5 us -> none  [local_step(): arrived = lax.all_to_all(packed, 'ep', 0, 2, tiled=True)]
    all_to_all x1 -> x0, waiting for transfers between devices: 47.2 us -> none  [local_step(): lax.all_to_all(expert_out.reshape(1, n_local, group_size * cap_rows, mode...]
    reduce_sum x2 -> x0, other arithmetic: 10.7 us -> none  [the longest x1 9.9 us: local_step(): jnp.sum(weights[:, :, None] * picked.astype(jnp.float32), axis=1)]
    gather x2 -> x0, local copies, waits for them, and re-layouts: 9.8 us -> none  [local_step(): jnp.take(returned.reshape(n_exp * cap_rows, model_dim), jnp.maximum(buf_p...]
    reshape x1 -> x0, local copies, waits for them, and re-layouts: 8.47 us -> none  [local_step(): expert_out.reshape(1, n_local, group_size * cap_rows, model_dim)]
    all_to_all x2 -> x0, local copies, waits for them, and re-layouts: 6.55 us -> none  [the longest x1 6.03 us: local_step(): lax.all_to_all(expert_out.reshape(1, n_local, group_size * cap_rows, mode...]
  transfers between devices with their start and end apart: 1 -> 0, of which waited for: 1 -> 0; matrix products, arithmetic and copies ran while one was open for 0% -> 0% of each run, Pallas kernels for 0% -> 0%
where the time goes in v3:
time: 108 us; the launch traced here: 107 us
  Pallas kernels  105 us (97%)
  local copies, waits for them, and re-layouts  2.3 us (2%)
    pallas_call x1, Pallas kernels, local_step(): pl.pallas_call(kernel, name='moe', out_shape=jax.ShapeDtypeStruct((tok_n,...  105 us
    unnamed x1, local copies, waits for them, and re-layouts  2.3 us

profile of v3, /device:TPU:0, one launch (start us, length us, event | category | flops | bytes accessed | tf_op | source)
XLA Modules:
  0.0 107.2 jit_solution(17778063875794143447)
XLA Ops:
  0.0 104.9 %moe.1 = bf16[256,2048]{1,0:T(8,128)(2,1)} custom-call(bf16[256,2048]{1,0:T(8,128)(2,1)} %tok_hbm.1, s32[2,256]{1,0:T(2,128)} %bitcast.2, f32[2,256]{1,0:T(2,128)} %bitcast.3, s32[1,8]{1,0:T(1,128)} %cnt_ref.1, bf16[2,2048,5632]{2,1,0:T(8,128)(2,1)} %wg_hbm.1, bf16[2,2048,5632]{2,1,0:T(8,128)(2,1)} %wu_hbm.1, bf16[2,5632,2048]{2,1,0:T(8,128)(2,1)} %wd_hbm.1), custom_call_target="tpu_custom_call" | custom-call | tf_op jit(solution)/shard_map/moe/pallas_call | solution.py:287
  104.9 2.3 %copy.9 = bf16[256,2048]{1,0:T(8,128)(2,1)} copy(bf16[256,2048]{1,0:T(8,128)(2,1)} %moe.1) | data formatting | bytes 2097152

commit v4 on v3

v4 whole, which is shorter than its diff:
```python
import jax
import jax.numpy as jnp
from jax import lax
from jax.experimental import pallas as pl
from jax.experimental.pallas import tpu as pltpu
from jax.sharding import PartitionSpec as P

N_CHUNKS = 4
N_COLS = 4
GU_SLOTS = 8
DN_SLOTS = 6
F_BLOCK = 512
GROUPS = ((0, 4), (4, 8), (8, 11))
BF = jnp.bfloat16
F32 = jnp.float32
N_PHASE = 4
FOLDS = ((1, 0), (0, 0), (0, 1), (1, 1))
RECV = 8


def kernel(
    tok_hbm, ids_ref, gate_ref, cnt_ref, wg_hbm, wu_hbm, wd_hbm, out_hbm,
    buf, maps, gates, hid, acc, gu, dn,
    s_own, s_gu, s_dn, xs_send, xs_recv, ps_send, ps_recv, rs_send, rs_recv, ms_send, ms_recv, ys_send, ys_recv, s_out,
):
    _, cap, dim = tok_hbm.shape
    tok_n = 2 * cap
    ffn = wg_hbm.shape[2]
    n_gu = ffn // F_BLOCK
    chunk = tok_n // N_CHUNKS
    cw = dim // N_COLS
    hw = cw // 2

    me = lax.axis_index("ep")
    partner = me + 1 - 2 * (me % 2)
    across = (me + 2) % 4
    diagonal = (partner + 2) % 4
    devs = (me, partner, across, diagonal)

    def remote(src, dst, send, recv, dev):
        return pltpu.make_async_remote_copy(
            src_ref=src, dst_ref=dst, send_sem=send, recv_sem=recv,
            device_id={"ep": dev}, device_id_type=pl.DeviceIdType.MESH,
        )

    def gu_slot(exp, blk):
        return jnp.where(exp == 0, blk % GU_SLOTS, (GU_SLOTS - 1 + n_gu * GU_SLOTS - blk) % GU_SLOTS)

    def gu_copies(exp, blk):
        cols = pl.ds(pl.multiple_of(blk * F_BLOCK, F_BLOCK), F_BLOCK)
        slot = gu_slot(exp, blk)
        return (
            pltpu.make_async_copy(wg_hbm.at[exp, :, cols], gu.at[slot, 0], s_gu.at[slot, 0]),
            pltpu.make_async_copy(wu_hbm.at[exp, :, cols], gu.at[slot, 1], s_gu.at[slot, 1]),
        )

    def gu_start(exp, blks):
        for blk in blks:
            for c in gu_copies(exp, blk):
                c.start()

    def dn_copy(h):
        cols = pl.ds(pl.multiple_of((h % (2 * N_COLS)) * hw, hw), hw)
        slot = h % DN_SLOTS
        return pltpu.make_async_copy(wd_hbm.at[h // (4 * N_COLS), :, cols], dn.at[slot], s_dn.at[slot])

    def dn_start(h):
        dn_copy(h).start()
        dn_copy(h + 1).start()

    own_copy = pltpu.make_async_copy(tok_hbm, buf.at[pl.ds(0, 2)], s_own)
    own_copy.start()
    gu_start(0, range(4))

    barrier = pltpu.get_barrier_semaphore()
    for peer in (1, 2, 3):
        pl.semaphore_signal(barrier, inc=1, device_id={"ep": devs[peer]}, device_id_type=pl.DeviceIdType.MESH)
    pl.semaphore_wait(barrier, 3)

    def rows_of(peer, c):
        return buf.at[2 * peer + c // (N_CHUNKS // 2), pl.ds(c % (N_CHUNKS // 2) * chunk, chunk)]

    x_copies = [
        remote(tok_hbm.at[c // (N_CHUNKS // 2), pl.ds(c % (N_CHUNKS // 2) * chunk, chunk)], rows_of(2, c), xs_send.at[c], xs_recv.at[c], across)
        for c in range(N_CHUNKS)
    ]
    r_copies = [remote(rows_of(2, c), rows_of(3, c), rs_send.at[c], rs_recv.at[c], partner) for c in range(N_CHUNKS)]
    p_copy = remote(tok_hbm, buf.at[pl.ds(2, 2)], ps_send, ps_recv, partner)
    x_copies[0].start()
    p_copy.start()
    for c in range(1, N_CHUNKS):
        x_copies[c].start()

    row = lax.broadcasted_iota(jnp.int32, (8, 1), 0)
    exp_row = row % 2 + 2 * jnp.where(row < 2, devs[0], jnp.where(row < 4, devs[1], jnp.where(row < 6, devs[2], devs[3])))
    hit0 = ids_ref[0:1, :] == exp_row
    hit1 = ids_ref[1:2, :] == exp_row
    hit = jnp.where(hit0 | hit1, 1.0, 0.0)
    earlier = jnp.where(
        lax.broadcasted_iota(jnp.int32, (tok_n, tok_n), 0) < lax.broadcasted_iota(jnp.int32, (tok_n, tok_n), 1), 1.0, 0.0
    ).astype(BF)
    slot = jnp.dot(hit.astype(BF), earlier, preferred_element_type=F32)
    limit = jnp.sum(jnp.where(exp_row == lax.broadcasted_iota(jnp.int32, (8, 8), 1), cnt_ref[...], 0), axis=1, keepdims=True)
    served = (hit > 0.0) & (slot < limit.astype(F32))
    slot1 = jnp.where(served, slot + 1.0, 0.0)
    maps[0] = slot1
    m_copies = [remote(maps.at[0], maps.at[r], ms_send.at[r - 1], ms_recv.at[r - 1], devs[r]) for r in (1, 2, 3)]
    for c in m_copies:
        c.start()
    gates_t = (jnp.where(hit0, gate_ref[0:1, :], 0.0) + jnp.where(hit1, gate_ref[1:2, :], 0.0)).T
    slot1_t = slot1.T
    for f, (exp, side) in enumerate(FOLDS):
        for half in range(2):
            i = 2 * (2 * side + half) + exp
            gates[f, :, half : half + 1] = gates_t[:, i : i + 1]
            gates[f, :, 2 + half : 3 + half] = slot1_t[:, i : i + 1]
    own_copy.wait()
    for k in range(N_COLS):
        for half in range(2):
            acc[half * cap : (half + 1) * cap, k * cw : (k + 1) * cw] = buf[half, :, k * cw : (k + 1) * cw].astype(F32)

    def relay(c):
        x_copies[c].wait_recv()
        r_copies[c].start()

    def y_copy(exp, peer, part, k, dev):
        cols = pl.ds(k * cw, cw)
        return remote(buf.at[part, :, cols], buf.at[RECV + 3 * exp + peer - 1, :, cols], ys_send.at[exp, peer, k], ys_recv.at[exp, peer, k], dev)

    def folded(f, base_slot, srcs, k):
        total = acc[:, k * cw : (k + 1) * cw]
        lane = (lax.broadcasted_iota(jnp.int32, (tok_n, cap), 1) + base_slot).astype(F32)
        for half in range(2):
            comb = jnp.where(gates[f, :, 2 + half : 3 + half] == lane, 1.0, 0.0).astype(BF)
            picked = jnp.dot(comb, buf[srcs[half], :, k * cw : (k + 1) * cw], preferred_element_type=F32)
            total += gates[f, :, half : half + 1] * picked
        return total

    def gather(side):
        slots = lax.broadcasted_iota(jnp.int32, (cap, tok_n), 0).astype(F32) + 1.0
        picks = [
            [
                jnp.where(maps[2 * side + half, pl.ds(2 * (2 * side + half) + exp, 1), :] == slots, 1.0, 0.0).astype(BF)
                for half in range(2)
            ]
            for exp in range(2)
        ]
        for k in range(N_COLS):
            cols = slice(k * cw, (k + 1) * cw)
            toks = [buf[pl.ds(4 * side + 2 * half, 2), :, cols].reshape(tok_n, cw) for half in range(2)]
            got = [[jnp.dot(picks[exp][half], toks[half], preferred_element_type=F32).astype(BF) for half in range(2)] for exp in range(2)]
            for exp in range(2):
                for half in range(2):
                    buf[4 * side + 2 * (1 - exp) + half, :, cols] = got[exp][half]

    def phase_step(p, carry):
        exp = p // 2
        rev = p % 2
        side = ((p + 1) // 2) % 2
        base = jnp.where(side == 0, me, across)
        base_partner = jnp.where(side == 0, partner, diagonal)

        work = 4 * side + 2 * (1 - exp)

        @pl.when(p == 0)
        def _():
            p_copy.wait_recv()
            m_copies[0].wait_recv()

        @pl.when(p == 1)
        def _():
            m_copies[1].wait_recv()
            m_copies[2].wait_recv()
            for c in r_copies:
                c.wait_recv()
                c.wait_send()

        @pl.when(p < 2)
        def _():
            gather(side)

        def blk_of(s):
            return s + rev * (n_gu - 1 - 2 * s)

        for n, (first, last) in enumerate(GROUPS):
            @pl.when((rev == 0) | (n == 2))
            def _():
                for s in range(first, last):
                    for c in gu_copies(exp, blk_of(s)):
                        c.wait()

            @pl.when(p == 0)
            def _():
                if n == 0:
                    gu_start(0, range(4, 8))
                elif n == 1:
                    gu_start(0, range(8, n_gu))
                    dn_start(0)
                else:
                    dn_start(2)
                    relay(0)

            if n == 1:
                @pl.when(p == 1)
                def _():
                    gu_start(0, (2, 1, 0))
                    gu_start(1, (0,))

                @pl.when(p == 2)
                def _():
                    gu_start(1, (8, 9, 10))

                @pl.when(p == 3)
                def _():
                    gu_start(1, (2, 1, 0))
            elif n == 2:
                dn_start(p * 2 * N_COLS + 4)

                @pl.when(p == 1)
                def _():
                    gu_start(1, (1, 2, 3))

            rows = buf.at[pl.ds(work, 2)]
            for s in range(first, last):
                sl = gu_slot(exp, blk_of(s))
                a = jnp.dot(rows[...].reshape(tok_n, dim), gu[sl, 0], preferred_element_type=F32)
                b = jnp.dot(rows[...].reshape(tok_n, dim), gu[sl, 1], preferred_element_type=F32)
                hid[:, pl.ds(pl.multiple_of(blk_of(s) * F_BLOCK, F_BLOCK), F_BLOCK)] = (a * jax.nn.sigmoid(a) * b).astype(BF)

        f_exp = p // 3
        f_side = p // 2
        base_slot = jnp.where(p == 0, tok_n, 1)
        src0 = jnp.where(p == 0, 0, jnp.where(p == 1, 2, RECV + 3 * f_exp + 1))
        src1 = jnp.where(p == 0, 0, RECV + 3 * f_exp + 2 * f_side)
        for k in range(N_COLS):
            h = 2 * (p * N_COLS + k)
            for i in range(2):
                dn_copy(h + i).wait()

            @pl.when(p > 0)
            def _():
                y_copy(f_exp, 2 * f_side + 1, 0, k, me).wait_recv()

            @pl.when(p > 1)
            def _():
                y_copy(f_exp, 2, 0, k, me).wait_recv()

            if k > 0:
                @pl.when(h + 4 < 2 * N_PHASE * N_COLS)
                def _():
                    dn_start(h + 4)

            if k > 1:
                @pl.when(p == 1)
                def _():
                    gu_start(1, (2 * k, 2 * k + 1))

            if k != 1:
                @pl.when(p == 0)
                def _():
                    relay(max(k, 1))

            acc[:, k * cw : (k + 1) * cw] = folded(p, base_slot, (src0, src1), k)
            for i in range(2):
                y = jnp.dot(hid[...], dn[(h + i) % DN_SLOTS], preferred_element_type=F32).astype(BF)
                for half in range(2):
                    buf[work + half, :, k * cw + i * hw : k * cw + (i + 1) * hw] = y[half * cap : (half + 1) * cap]
            y_copy(exp, 2 * side + 1, work + 1, k, base_partner).start()

            @pl.when(side == 1)
            def _():
                y_copy(exp, 2, work, k, base).start()
        return carry

    lax.fori_loop(0, N_PHASE, phase_step, 0)

    for k in range(N_COLS):
        y_copy(0, 1, 3, k, partner).wait_send()
    outs = []
    for k in range(N_COLS):
        y_copy(1, 1, 1, k, partner).wait_recv()
        cols = slice(k * cw, (k + 1) * cw)
        total = folded(0, 1, (0, RECV + 3), k).astype(BF)
        for half in range(2):
            buf[2 + half, :, cols] = total[half * cap : (half + 1) * cap]
        outs.append(pltpu.make_async_copy(buf.at[pl.ds(2, 2), :, cols], out_hbm.at[:, :, cols], s_out.at[k]))
        outs[k].start()

    for c in x_copies + m_copies + [p_copy]:
        c.wait_send()
    for exp in range(2):
        for peer in range(1, 4):
            for k in range(N_COLS):
                if exp + peer > 1:
                    y_copy(exp, peer, 0, k, devs[peer]).wait_send()
    for c in outs:
        c.wait()


def solution(mesh):
    row_spec = P(("dp", "ep"))

    def local_step(tokens, expert_ids, gate_w, route_counts, w_gate, w_up, w_down):
        tok_n, dim = tokens.shape
        ffn = w_gate.shape[2]
        cap = tok_n // 2
        cw = dim // N_COLS
        vmem = pl.BlockSpec(memory_space=pltpu.VMEM)
        hbm = pl.BlockSpec(memory_space=pl.ANY)
        dma = pltpu.SemaphoreType.DMA
        return pl.pallas_call(
            kernel,
            name="moe",
            out_shape=jax.ShapeDtypeStruct((2, cap, dim), BF),
            in_specs=[hbm, vmem, vmem, vmem, hbm, hbm, hbm],
            out_specs=hbm,
            scratch_shapes=[
                pltpu.VMEM((RECV + 6, cap, dim), BF),
                pltpu.VMEM((4, 8, tok_n), F32),
                pltpu.VMEM((4, tok_n, 4), F32),
                pltpu.VMEM((2 * cap, ffn), BF),
                pltpu.VMEM((tok_n, dim), F32),
                pltpu.VMEM((GU_SLOTS, 2, dim, F_BLOCK), BF),
                pltpu.VMEM((DN_SLOTS, ffn, cw // 2), BF),
                dma, dma((GU_SLOTS, 2)), dma((DN_SLOTS,)),
                dma((N_CHUNKS,)), dma((N_CHUNKS,)), dma, dma,
                dma((N_CHUNKS,)), dma((N_CHUNKS,)), dma((3,)), dma((3,)),
                dma((2, 4, N_COLS)), dma((2, 4, N_COLS)), dma((N_COLS,)),
            ],
            compiler_params=pltpu.CompilerParams(
                collective_id=0, has_side_effects=True, vmem_limit_bytes=67_000_000
            ),
        )(tokens.reshape(2, cap, dim), expert_ids.T, gate_w.T, route_counts, w_gate, w_up, w_down).reshape(tok_n, dim)

    return jax.shard_map(local_step, mesh=mesh, in_specs=(row_spec, row_spec, row_spec, row_spec, P("ep"), P("ep"), P("ep")), out_specs=row_spec, check_vma=False)
```

time: 108 us -> 101 us (0.935)
  Pallas kernels: 105 us -> 98.2 us
    pallas_call x1, Pallas kernels: 105 us -> 98.2 us  [local_step(): pl.pallas_call(kernel, name='moe', out_shape=jax.ShapeDtypeStruct((2, cap...]
where the time goes in v4:
time: 101 us
  Pallas kernels  98.2 us (97%)
  local copies, waits for them, and re-layouts  2.3 us (2%)
    pallas_call x1, Pallas kernels, local_step(): pl.pallas_call(kernel, name='moe', out_shape=jax.ShapeDtypeStruct((2, cap...  98.2 us
    unnamed x1, local copies, waits for them, and re-layouts  2.3 us

profile of v4, /device:TPU:0, one launch (start us, length us, event | category | flops | bytes accessed | tf_op | source)
XLA Modules:
  0.0 100.5 jit_solution(7418885621366479799)
XLA Ops:
  0.0 98.2 %moe.1 = bf16[2,128,2048]{2,1,0:T(8,128)(2,1)} custom-call(bf16[2,128,2048]{2,1,0:T(8,128)(2,1)} %bitcast.5, s32[2,256]{1,0:T(2,128)} %bitcast.6, f32[2,256]{1,0:T(2,128)} %bitcast.7, s32[1,8]{1,0:T(1,128)} %cnt_ref.1, bf16[2,2048,5632]{2,1,0:T(8,128)(2,1)} %wg_hbm.1, bf16[2,2048,5632]{2,1,0:T(8,128)(2,1)} %wu_hbm.1, bf16[2,5632,2048]{2,1,0:T(8,128)(2,1)} %wd_hbm.1), custom_call_target="tpu_custom_call" | custom-call | tf_op jit(solution)/shard_map/moe/pallas_call | solution.py:311
  98.2 2.3 %copy.9 = bf16[256,2048]{1,0:T(8,128)(2,1)} copy(bf16[256,2048]{1,0:T(8,128)(2,1)} %bitcast.4) | data formatting | bytes 2097152

commit v5 on v4

--- a/solution.py
+++ b/solution.py
@@ -10,7 +10,7 @@
 GU_SLOTS = 8
 DN_SLOTS = 6
 F_BLOCK = 512
-GROUPS = ((0, 4), (4, 8), (8, 11))
+GROUPS = ((0, 2), (2, 5), (5, 8), (8, 11))
 BF = jnp.bfloat16
 F32 = jnp.float32
 N_PHASE = 4
@@ -70,7 +70,7 @@
 
     own_copy = pltpu.make_async_copy(tok_hbm, buf.at[pl.ds(0, 2)], s_own)
     own_copy.start()
-    gu_start(0, range(4))
+    gu_start(0, range(2))
 
     barrier = pltpu.get_barrier_semaphore()
     for peer in (1, 2, 3):
@@ -115,6 +115,7 @@
             gates[f, :, half : half + 1] = gates_t[:, i : i + 1]
             gates[f, :, 2 + half : 3 + half] = slot1_t[:, i : i + 1]
     own_copy.wait()
+    gu_start(0, range(2, 5))
     for k in range(N_COLS):
         for half in range(2):
             acc[half * cap : (half + 1) * cap, k * cw : (k + 1) * cw] = buf[half, :, k * cw : (k + 1) * cw].astype(F32)
@@ -127,8 +128,8 @@
         cols = pl.ds(k * cw, cw)
         return remote(buf.at[part, :, cols], buf.at[RECV + 3 * exp + peer - 1, :, cols], ys_send.at[exp, peer, k], ys_recv.at[exp, peer, k], dev)
 
-    def folded(f, base_slot, srcs, k):
-        total = acc[:, k * cw : (k + 1) * cw]
+    def folded(f, base_slot, srcs, k, total=None):
+        total = acc[:, k * cw : (k + 1) * cw] if total is None else total
         lane = (lax.broadcasted_iota(jnp.int32, (tok_n, cap), 1) + base_slot).astype(F32)
         for half in range(2):
             comb = jnp.where(gates[f, :, 2 + half : 3 + half] == lane, 1.0, 0.0).astype(BF)
@@ -183,7 +184,7 @@
             return s + rev * (n_gu - 1 - 2 * s)
 
         for n, (first, last) in enumerate(GROUPS):
-            @pl.when((rev == 0) | (n == 2))
+            @pl.when((rev == 0) | (n == 3))
             def _():
                 for s in range(first, last):
                     for c in gu_copies(exp, blk_of(s)):
@@ -192,33 +193,42 @@
             @pl.when(p == 0)
             def _():
                 if n == 0:
-                    gu_start(0, range(4, 8))
+                    gu_start(0, (5, 6, 7))
                 elif n == 1:
-                    gu_start(0, range(8, n_gu))
+                    gu_start(0, (8, 9))
+                elif n == 2:
+                    gu_start(0, (10,))
                     dn_start(0)
                 else:
                     dn_start(2)
                     relay(0)
 
-            if n == 1:
-                @pl.when(p == 1)
-                def _():
-                    gu_start(0, (2, 1, 0))
+            @pl.when(p == 1)
+            def _():
+                if n == 1:
+                    gu_start(0, (2, 1))
+                elif n == 2:
+                    gu_start(0, (0,))
+                    gu_start(1, (0, 1))
+                elif n == 3:
+                    gu_start(1, (2, 3, 4))
+
+            @pl.when(p == 2)
+            def _():
+                if n == 1:
+                    gu_start(1, (8, 9))
+                elif n == 2:
+                    gu_start(1, (10,))
+
+            @pl.when(p == 3)
+            def _():
+                if n == 1:
+                    gu_start(1, (2, 1))
+                elif n == 2:
                     gu_start(1, (0,))
 
-                @pl.when(p == 2)
-                def _():
-                    gu_start(1, (8, 9, 10))
-
-                @pl.when(p == 3)
-                def _():
-                    gu_start(1, (2, 1, 0))
-            elif n == 2:
+            if n == 3:
                 dn_start(p * 2 * N_COLS + 4)
-
-                @pl.when(p == 1)
-                def _():
-                    gu_start(1, (1, 2, 3))
 
             rows = buf.at[pl.ds(work, 2)]
             for s in range(first, last):
@@ -227,23 +237,26 @@
                 b = jnp.dot(rows[...].reshape(tok_n, dim), gu[sl, 1], preferred_element_type=F32)
                 hid[:, pl.ds(pl.multiple_of(blk_of(s) * F_BLOCK, F_BLOCK), F_BLOCK)] = (a * jax.nn.sigmoid(a) * b).astype(BF)
 
-        f_exp = p // 3
-        f_side = p // 2
-        base_slot = jnp.where(p == 0, tok_n, 1)
-        src0 = jnp.where(p == 0, 0, jnp.where(p == 1, 2, RECV + 3 * f_exp + 1))
-        src1 = jnp.where(p == 0, 0, RECV + 3 * f_exp + 2 * f_side)
         for k in range(N_COLS):
             h = 2 * (p * N_COLS + k)
             for i in range(2):
                 dn_copy(h + i).wait()
 
-            @pl.when(p > 0)
-            def _():
-                y_copy(f_exp, 2 * f_side + 1, 0, k, me).wait_recv()
-
-            @pl.when(p > 1)
-            def _():
-                y_copy(f_exp, 2, 0, k, me).wait_recv()
+            f = p if k > 0 else p - 1
+            kf = (k - 1) % N_COLS
+            f_exp = jnp.where(f == 3, 1, 0)
+            f_side = jnp.where(f >= 2, 1, 0)
+            base_slot = jnp.where(f >= 1, 1, tok_n)
+            src0 = jnp.where(f < 1, 0, jnp.where(f == 1, 2, RECV + 3 * f_exp + 1))
+            src1 = jnp.where(f < 1, 0, RECV + 3 * f_exp + 2 * f_side)
+
+            @pl.when(f >= 1)
+            def _():
+                y_copy(f_exp, 2 * f_side + 1, 0, kf, me).wait_recv()
+
+            @pl.when(f >= 2)
+            def _():
+                y_copy(f_exp, 2, 0, kf, me).wait_recv()
 
             if k > 0:
                 @pl.when(h + 4 < 2 * N_PHASE * N_COLS)
@@ -253,14 +266,14 @@
             if k > 1:
                 @pl.when(p == 1)
                 def _():
-                    gu_start(1, (2 * k, 2 * k + 1))
+                    gu_start(1, (5, 6) if k == 2 else (7,))
 
             if k != 1:
                 @pl.when(p == 0)
                 def _():
                     relay(max(k, 1))
 
-            acc[:, k * cw : (k + 1) * cw] = folded(p, base_slot, (src0, src1), k)
+            acc[:, kf * cw : (kf + 1) * cw] = folded(jnp.maximum(f, 0), base_slot, (src0, src1), kf)
             for i in range(2):
                 y = jnp.dot(hid[...], dn[(h + i) % DN_SLOTS], preferred_element_type=F32).astype(BF)
                 for half in range(2):
@@ -280,7 +293,12 @@
     for k in range(N_COLS):
         y_copy(1, 1, 1, k, partner).wait_recv()
         cols = slice(k * cw, (k + 1) * cw)
-        total = folded(0, 1, (0, RECV + 3), k).astype(BF)
+        total = None
+        if k == N_COLS - 1:
+            for peer in (2, 3):
+                y_copy(1, peer, 0, k, me).wait_recv()
+            total = folded(3, 1, (RECV + 4, RECV + 5), k)
+        total = folded(0, 1, (0, RECV + 3), k, total).astype(BF)
         for half in range(2):
             buf[2 + half, :, cols] = total[half * cap : (half + 1) * cap]
         outs.append(pltpu.make_async_copy(buf.at[pl.ds(2, 2), :, cols], out_hbm.at[:, :, cols], s_out.at[k]))

time: 101 us -> 97.3 us (0.963)
  Pallas kernels: 98.2 us -> 94.8 us
    pallas_call x1, Pallas kernels: 98.2 us -> 94.8 us  [local_step(): pl.pallas_call(kernel, name='moe', out_shape=jax.ShapeDtypeStruct((2, cap...]
where the time goes in v5:
time: 97.3 us; the launch traced here: 97.1 us
  Pallas kernels  94.8 us (97%)
  local copies, waits for them, and re-layouts  2.3 us (2%)
    pallas_call x1, Pallas kernels, local_step(): pl.pallas_call(kernel, name='moe', out_shape=jax.ShapeDtypeStruct((2, cap...  94.8 us
    unnamed x1, local copies, waits for them, and re-layouts  2.3 us

profile of v5, /device:TPU:0, one launch (start us, length us, event | category | flops | bytes accessed | tf_op | source)
XLA Modules:
  0.0 97.1 jit_solution(8294047332585724556)
XLA Ops:
  0.0 94.8 %moe.1 = bf16[2,128,2048]{2,1,0:T(8,128)(2,1)} custom-call(bf16[2,128,2048]{2,1,0:T(8,128)(2,1)} %bitcast.5, s32[2,256]{1,0:T(2,128)} %bitcast.6, f32[2,256]{1,0:T(2,128)} %bitcast.7, s32[1,8]{1,0:T(1,128)} %cnt_ref.1, bf16[2,2048,5632]{2,1,0:T(8,128)(2,1)} %wg_hbm.1, bf16[2,2048,5632]{2,1,0:T(8,128)(2,1)} %wu_hbm.1, bf16[2,5632,2048]{2,1,0:T(8,128)(2,1)} %wd_hbm.1), custom_call_target="tpu_custom_call" | custom-call | tf_op jit(solution)/shard_map/moe/pallas_call | solution.py:329
  94.8 2.3 %copy.9 = bf16[256,2048]{1,0:T(8,128)(2,1)} copy(bf16[256,2048]{1,0:T(8,128)(2,1)} %bitcast.4) | data formatting | bytes 2097152

commit v6 on v5

--- a/solution.py
+++ b/solution.py
@@ -19,9 +19,9 @@
 
 
 def kernel(
-    tok_hbm, ids_ref, gate_ref, cnt_ref, wg_hbm, wu_hbm, wd_hbm, out_hbm,
-    buf, maps, gates, hid, acc, gu, dn,
-    s_own, s_gu, s_dn, xs_send, xs_recv, ps_send, ps_recv, rs_send, rs_recv, ms_send, ms_recv, ys_send, ys_recv, s_out,
+    tok_hbm, ids_ref, gate_ref, cnt_ref, wg_hbm, wu_hbm, wd_hbm, acc,
+    buf, maps, gates, hid, gu, dn,
+    s_own, s_gu, s_dn, xs_send, xs_recv, ps_send, ps_recv, rs_send, rs_recv, ms_send, ms_recv, ys_send, ys_recv,
 ):
     _, cap, dim = tok_hbm.shape
     tok_n = 2 * cap
@@ -128,14 +128,16 @@
         cols = pl.ds(k * cw, cw)
         return remote(buf.at[part, :, cols], buf.at[RECV + 3 * exp + peer - 1, :, cols], ys_send.at[exp, peer, k], ys_recv.at[exp, peer, k], dev)
 
-    def folded(f, base_slot, srcs, k, total=None):
-        total = acc[:, k * cw : (k + 1) * cw] if total is None else total
+    def fold(f, base_slot, srcs, k):
         lane = (lax.broadcasted_iota(jnp.int32, (tok_n, cap), 1) + base_slot).astype(F32)
-        for half in range(2):
-            comb = jnp.where(gates[f, :, 2 + half : 3 + half] == lane, 1.0, 0.0).astype(BF)
-            picked = jnp.dot(comb, buf[srcs[half], :, k * cw : (k + 1) * cw], preferred_element_type=F32)
-            total += gates[f, :, half : half + 1] * picked
-        return total
+        combs = [jnp.where(gates[f, :, 2 + half : 3 + half] == lane, 1.0, 0.0).astype(BF) for half in range(2)]
+        for i in range(2):
+            cols = slice(k * cw + i * hw, k * cw + (i + 1) * hw)
+            total = acc[:, cols]
+            for half in range(2):
+                picked = jnp.dot(combs[half], buf[srcs[half], :, cols], preferred_element_type=F32)
+                total += gates[f, :, half : half + 1] * picked
+            acc[:, cols] = total
 
     def gather(side):
         slots = lax.broadcasted_iota(jnp.int32, (cap, tok_n), 0).astype(F32) + 1.0
@@ -146,9 +148,9 @@
             ]
             for exp in range(2)
         ]
-        for k in range(N_COLS):
-            cols = slice(k * cw, (k + 1) * cw)
-            toks = [buf[pl.ds(4 * side + 2 * half, 2), :, cols].reshape(tok_n, cw) for half in range(2)]
+        for k in range(2 * N_COLS):
+            cols = slice(k * hw, (k + 1) * hw)
+            toks = [buf[pl.ds(4 * side + 2 * half, 2), :, cols].reshape(tok_n, hw) for half in range(2)]
             got = [[jnp.dot(picks[exp][half], toks[half], preferred_element_type=F32).astype(BF) for half in range(2)] for exp in range(2)]
             for exp in range(2):
                 for half in range(2):
@@ -233,9 +235,12 @@
             rows = buf.at[pl.ds(work, 2)]
             for s in range(first, last):
                 sl = gu_slot(exp, blk_of(s))
-                a = jnp.dot(rows[...].reshape(tok_n, dim), gu[sl, 0], preferred_element_type=F32)
-                b = jnp.dot(rows[...].reshape(tok_n, dim), gu[sl, 1], preferred_element_type=F32)
-                hid[:, pl.ds(pl.multiple_of(blk_of(s) * F_BLOCK, F_BLOCK), F_BLOCK)] = (a * jax.nn.sigmoid(a) * b).astype(BF)
+                for i in range(2):
+                    cols = slice(i * hw, (i + 1) * hw)
+                    a = jnp.dot(rows[...].reshape(tok_n, dim), gu[sl, 0, :, cols], preferred_element_type=F32)
+                    b = jnp.dot(rows[...].reshape(tok_n, dim), gu[sl, 1, :, cols], preferred_element_type=F32)
+                    off = pl.multiple_of(blk_of(s) * F_BLOCK, F_BLOCK) + i * hw
+                    hid[:, pl.ds(pl.multiple_of(off, hw), hw)] = (a * jax.nn.sigmoid(a) * b).astype(BF)
 
         for k in range(N_COLS):
             h = 2 * (p * N_COLS + k)
@@ -273,7 +278,7 @@
                 def _():
                     relay(max(k, 1))
 
-            acc[:, kf * cw : (kf + 1) * cw] = folded(jnp.maximum(f, 0), base_slot, (src0, src1), kf)
+            fold(jnp.maximum(f, 0), base_slot, (src0, src1), kf)
             for i in range(2):
                 y = jnp.dot(hid[...], dn[(h + i) % DN_SLOTS], preferred_element_type=F32).astype(BF)
                 for half in range(2):
@@ -288,31 +293,19 @@
     lax.fori_loop(0, N_PHASE, phase_step, 0)
 
     for k in range(N_COLS):
-        y_copy(0, 1, 3, k, partner).wait_send()
-    outs = []
-    for k in range(N_COLS):
         y_copy(1, 1, 1, k, partner).wait_recv()
-        cols = slice(k * cw, (k + 1) * cw)
-        total = None
         if k == N_COLS - 1:
             for peer in (2, 3):
                 y_copy(1, peer, 0, k, me).wait_recv()
-            total = folded(3, 1, (RECV + 4, RECV + 5), k)
-        total = folded(0, 1, (0, RECV + 3), k, total).astype(BF)
-        for half in range(2):
-            buf[2 + half, :, cols] = total[half * cap : (half + 1) * cap]
-        outs.append(pltpu.make_async_copy(buf.at[pl.ds(2, 2), :, cols], out_hbm.at[:, :, cols], s_out.at[k]))
-        outs[k].start()
+            fold(3, 1, (RECV + 4, RECV + 5), k)
+        fold(0, 1, (0, RECV + 3), k)
 
     for c in x_copies + m_copies + [p_copy]:
         c.wait_send()
     for exp in range(2):
         for peer in range(1, 4):
             for k in range(N_COLS):
-                if exp + peer > 1:
-                    y_copy(exp, peer, 0, k, devs[peer]).wait_send()
-    for c in outs:
-        c.wait()
+                y_copy(exp, peer, 0, k, devs[peer]).wait_send()
 
 
 def solution(mesh):
@@ -329,25 +322,24 @@
         return pl.pallas_call(
             kernel,
             name="moe",
-            out_shape=jax.ShapeDtypeStruct((2, cap, dim), BF),
+            out_shape=pltpu.VMEM((tok_n, dim), F32),
             in_specs=[hbm, vmem, vmem, vmem, hbm, hbm, hbm],
-            out_specs=hbm,
+            out_specs=vmem,
             scratch_shapes=[
                 pltpu.VMEM((RECV + 6, cap, dim), BF),
                 pltpu.VMEM((4, 8, tok_n), F32),
                 pltpu.VMEM((4, tok_n, 4), F32),
                 pltpu.VMEM((2 * cap, ffn), BF),
-                pltpu.VMEM((tok_n, dim), F32),
                 pltpu.VMEM((GU_SLOTS, 2, dim, F_BLOCK), BF),
                 pltpu.VMEM((DN_SLOTS, ffn, cw // 2), BF),
                 dma, dma((GU_SLOTS, 2)), dma((DN_SLOTS,)),
                 dma((N_CHUNKS,)), dma((N_CHUNKS,)), dma, dma,
                 dma((N_CHUNKS,)), dma((N_CHUNKS,)), dma((3,)), dma((3,)),
-                dma((2, 4, N_COLS)), dma((2, 4, N_COLS)), dma((N_COLS,)),
+                dma((2, 4, N_COLS)), dma((2, 4, N_COLS)),
             ],
             compiler_params=pltpu.CompilerParams(
-                collective_id=0, has_side_effects=True, vmem_limit_bytes=67_000_000
+                collective_id=0, has_side_effects=True, vmem_limit_bytes=64_900_000
             ),
-        )(tokens.reshape(2, cap, dim), expert_ids.T, gate_w.T, route_counts, w_gate, w_up, w_down).reshape(tok_n, dim)
+        )(tokens.reshape(2, cap, dim), expert_ids.T, gate_w.T, route_counts, w_gate, w_up, w_down).astype(BF)
 
     return jax.shard_map(local_step, mesh=mesh, in_specs=(row_spec, row_spec, row_spec, row_spec, P("ep"), P("ep"), P("ep")), out_specs=row_spec, check_vma=False)

time: 97.3 us -> 95.9 us (0.986)
  local copies, waits for them, and re-layouts: 2.3 us -> 0 us
  other arithmetic: 0 us -> 1.12 us
    unnamed x1 -> x0, local copies, waits for them, and re-layouts: 2.3 us -> none
    convert_element_type x0 -> x1, other arithmetic: none -> 1.12 us  [local_step(): return pl.pallas_call(kernel, name='moe', out_shape=pltpu.VMEM((tok_n, di...]
where the time goes in v6:
time: 95.9 us; the launch traced here: 95.8 us
  Pallas kernels  94.7 us (99%)
  other arithmetic  1.12 us (1%)
    pallas_call x1, Pallas kernels, local_step(): pl.pallas_call(kernel, name='moe', out_shape=pltpu.VMEM((tok_n, dim), F32...  94.7 us

profile of v6, /device:TPU:0, one launch (start us, length us, event | category | flops | bytes accessed | tf_op | source)
XLA Modules:
  0.0 95.8 jit_solution(192378737252800145)
XLA Ops:
  0.0 94.7 %moe.1 = f32[256,2048]{1,0:T(8,128)S(1)} custom-call(bf16[2,128,2048]{2,1,0:T(8,128)(2,1)} %bitcast.3, s32[2,256]{1,0:T(2,128)} %bitcast.4, f32[2,256]{1,0:T(2,128)} %bitcast.5, s32[1,8]{1,0:T(1,128)} %cnt_ref.1, bf16[2,2048,5632]{2,1,0:T(8,128)(2,1)} %wg_hbm.1, bf16[2,2048,5632]{2,1,0:T(8,128)(2,1)} %wu_hbm.1, bf16[2,5632,2048]{2,1,0:T(8,128)(2,1)} %wd_hbm.1), custom_call_target="tpu_custom_call" | custom-call | tf_op jit(solution)/shard_map/moe/pallas_call | solution.py:322
  94.7 1.1 %convert_element_type.3 = bf16[256,2048]{1,0:T(8,128)(2,1)} convert(f32[256,2048]{1,0:T(8,128)S(1)} %moe.1) | non-fusion elementwise | flops 524288 | bytes 3145728 | tf_op jit(solution)/shard_map/convert_element_type | solution.py:343

commit v7 on v6

--- a/solution.py
+++ b/solution.py
@@ -5,7 +5,7 @@
 from jax.experimental.pallas import tpu as pltpu
 from jax.sharding import PartitionSpec as P
 
-N_CHUNKS = 4
+N_CHUNKS = 8
 N_COLS = 4
 GU_SLOTS = 8
 DN_SLOTS = 6
@@ -203,7 +203,8 @@
                     dn_start(0)
                 else:
                     dn_start(2)
-                    relay(0)
+                    for c in range(3):
+                        relay(c)
 
             @pl.when(p == 1)
             def _():
@@ -273,10 +274,10 @@
                 def _():
                     gu_start(1, (5, 6) if k == 2 else (7,))
 
-            if k != 1:
-                @pl.when(p == 0)
-                def _():
-                    relay(max(k, 1))
+            @pl.when(p == 0)
+            def _():
+                for c in ((3,), (4,), (5, 6), (7,))[k]:
+                    relay(c)
 
             fold(jnp.maximum(f, 0), base_slot, (src0, src1), kf)
             for i in range(2):
@@ -292,20 +293,24 @@
 
     lax.fori_loop(0, N_PHASE, phase_step, 0)
 
+    for c in x_copies + m_copies + [p_copy]:
+        c.wait_send()
+
+    def sent(exp, peer):
+        for k in range(N_COLS):
+            y_copy(exp, peer, 0, k, devs[peer]).wait_send()
+
+    for peer in range(1, 4):
+        sent(0, peer)
     for k in range(N_COLS):
         y_copy(1, 1, 1, k, partner).wait_recv()
-        if k == N_COLS - 1:
-            for peer in (2, 3):
-                y_copy(1, peer, 0, k, me).wait_recv()
-            fold(3, 1, (RECV + 4, RECV + 5), k)
         fold(0, 1, (0, RECV + 3), k)
-
-    for c in x_copies + m_copies + [p_copy]:
-        c.wait_send()
-    for exp in range(2):
-        for peer in range(1, 4):
-            for k in range(N_COLS):
-                y_copy(exp, peer, 0, k, devs[peer]).wait_send()
+    sent(1, 1)
+    for peer in (2, 3):
+        y_copy(1, peer, 0, N_COLS - 1, me).wait_recv()
+    fold(3, 1, (RECV + 4, RECV + 5), N_COLS - 1)
+    for peer in (2, 3):
+        sent(1, peer)
 
 
 def solution(mesh):

time: 95.9 us -> 96.3 us (level)
  no operation moved by 1% of the time
where the time goes in v7:
time: 96.3 us; the launch traced here: 96.2 us
  Pallas kernels  95.1 us (99%)
  other arithmetic  1.12 us (1%)
    pallas_call x1, Pallas kernels, local_step(): pl.pallas_call(kernel, name='moe', out_shape=pltpu.VMEM((tok_n, dim), F32...  95.1 us

profile of v7, /device:TPU:0, one launch (start us, length us, event | category | flops | bytes accessed | tf_op | source)
XLA Modules:
  0.0 96.2 jit_solution(14342027224797198337)
XLA Ops:
  0.0 95.1 %moe.1 = f32[256,2048]{1,0:T(8,128)S(1)} custom-call(bf16[2,128,2048]{2,1,0:T(8,128)(2,1)} %bitcast.3, s32[2,256]{1,0:T(2,128)} %bitcast.4, f32[2,256]{1,0:T(2,128)} %bitcast.5, s32[1,8]{1,0:T(1,128)} %cnt_ref.1, bf16[2,2048,5632]{2,1,0:T(8,128)(2,1)} %wg_hbm.1, bf16[2,2048,5632]{2,1,0:T(8,128)(2,1)} %wu_hbm.1, bf16[2,5632,2048]{2,1,0:T(8,128)(2,1)} %wd_hbm.1), custom_call_target="tpu_custom_call" | custom-call | tf_op jit(solution)/shard_map/moe/pallas_call | solution.py:327
  95.1 1.1 %convert_element_type.3 = bf16[256,2048]{1,0:T(8,128)(2,1)} convert(f32[256,2048]{1,0:T(8,128)S(1)} %moe.1) | non-fusion elementwise | flops 524288 | bytes 3145728 | tf_op jit(solution)/shard_map/convert_element_type | solution.py:348

commit v8 on v6

--- a/solution.py
+++ b/solution.py
@@ -20,7 +20,7 @@
 
 def kernel(
     tok_hbm, ids_ref, gate_ref, cnt_ref, wg_hbm, wu_hbm, wd_hbm, acc,
-    buf, maps, gates, hid, gu, dn,
+    buf, maps, comb, gates, hid, gu, dn,
     s_own, s_gu, s_dn, xs_send, xs_recv, ps_send, ps_recv, rs_send, rs_recv, ms_send, ms_recv, ys_send, ys_recv,
 ):
     _, cap, dim = tok_hbm.shape
@@ -109,11 +109,13 @@
         c.start()
     gates_t = (jnp.where(hit0, gate_ref[0:1, :], 0.0) + jnp.where(hit1, gate_ref[1:2, :], 0.0)).T
     slot1_t = slot1.T
+    lane = lax.broadcasted_iota(jnp.int32, (tok_n, cap), 1).astype(F32) + 1.0
+    comb[N_PHASE] = jnp.zeros((2, tok_n, cap), BF)
     for f, (exp, side) in enumerate(FOLDS):
         for half in range(2):
             i = 2 * (2 * side + half) + exp
             gates[f, :, half : half + 1] = gates_t[:, i : i + 1]
-            gates[f, :, 2 + half : 3 + half] = slot1_t[:, i : i + 1]
+            comb[f, half] = jnp.where(slot1_t[:, i : i + 1] == lane, 1.0, 0.0).astype(BF)
     own_copy.wait()
     gu_start(0, range(2, 5))
     for k in range(N_COLS):
@@ -128,14 +130,12 @@
         cols = pl.ds(k * cw, cw)
         return remote(buf.at[part, :, cols], buf.at[RECV + 3 * exp + peer - 1, :, cols], ys_send.at[exp, peer, k], ys_recv.at[exp, peer, k], dev)
 
-    def fold(f, base_slot, srcs, k):
-        lane = (lax.broadcasted_iota(jnp.int32, (tok_n, cap), 1) + base_slot).astype(F32)
-        combs = [jnp.where(gates[f, :, 2 + half : 3 + half] == lane, 1.0, 0.0).astype(BF) for half in range(2)]
+    def fold(f, c, srcs, k):
         for i in range(2):
             cols = slice(k * cw + i * hw, k * cw + (i + 1) * hw)
             total = acc[:, cols]
             for half in range(2):
-                picked = jnp.dot(combs[half], buf[srcs[half], :, cols], preferred_element_type=F32)
+                picked = jnp.dot(comb[c, half], buf[srcs[half], :, cols], preferred_element_type=F32)
                 total += gates[f, :, half : half + 1] * picked
             acc[:, cols] = total
 
@@ -251,7 +251,7 @@
             kf = (k - 1) % N_COLS
             f_exp = jnp.where(f == 3, 1, 0)
             f_side = jnp.where(f >= 2, 1, 0)
-            base_slot = jnp.where(f >= 1, 1, tok_n)
+            f_comb = jnp.where(f >= 1, f, N_PHASE)
             src0 = jnp.where(f < 1, 0, jnp.where(f == 1, 2, RECV + 3 * f_exp + 1))
             src1 = jnp.where(f < 1, 0, RECV + 3 * f_exp + 2 * f_side)
 
@@ -278,7 +278,7 @@
                 def _():
                     relay(max(k, 1))
 
-            fold(jnp.maximum(f, 0), base_slot, (src0, src1), kf)
+            fold(jnp.maximum(f, 0), f_comb, (src0, src1), kf)
             for i in range(2):
                 y = jnp.dot(hid[...], dn[(h + i) % DN_SLOTS], preferred_element_type=F32).astype(BF)
                 for half in range(2):
@@ -297,8 +297,8 @@
         if k == N_COLS - 1:
             for peer in (2, 3):
                 y_copy(1, peer, 0, k, me).wait_recv()
-            fold(3, 1, (RECV + 4, RECV + 5), k)
-        fold(0, 1, (0, RECV + 3), k)
+            fold(3, 3, (RECV + 4, RECV + 5), k)
+        fold(0, 0, (0, RECV + 3), k)
 
     for c in x_copies + m_copies + [p_copy]:
         c.wait_send()
@@ -328,7 +328,8 @@
             scratch_shapes=[
                 pltpu.VMEM((RECV + 6, cap, dim), BF),
                 pltpu.VMEM((4, 8, tok_n), F32),
-                pltpu.VMEM((4, tok_n, 4), F32),
+                pltpu.VMEM((N_PHASE + 1, 2, tok_n, cap), BF),
+                pltpu.VMEM((4, tok_n, 2), F32),
                 pltpu.VMEM((2 * cap, ffn), BF),
                 pltpu.VMEM((GU_SLOTS, 2, dim, F_BLOCK), BF),
                 pltpu.VMEM((DN_SLOTS, ffn, cw // 2), BF),

time: 95.9 us -> 95 us (level)
  no operation moved by 1% of the time
where the time goes in v8:
time: 95 us; the launch traced here: 94.9 us
  Pallas kernels  93.8 us (99%)
  other arithmetic  1.12 us (1%)
    pallas_call x1, Pallas kernels, local_step(): pl.pallas_call(kernel, name='moe', out_shape=pltpu.VMEM((tok_n, dim), F32...  93.8 us

profile of v8, /device:TPU:0, one launch (start us, length us, event | category | flops | bytes accessed | tf_op | source)
XLA Modules:
  0.0 94.9 jit_solution(7393201712355378847)
XLA Ops:
  0.0 93.8 %moe.1 = f32[256,2048]{1,0:T(8,128)S(1)} custom-call(bf16[2,128,2048]{2,1,0:T(8,128)(2,1)} %bitcast.3, s32[2,256]{1,0:T(2,128)} %bitcast.4, f32[2,256]{1,0:T(2,128)} %bitcast.5, s32[1,8]{1,0:T(1,128)} %cnt_ref.1, bf16[2,2048,5632]{2,1,0:T(8,128)(2,1)} %wg_hbm.1, bf16[2,2048,5632]{2,1,0:T(8,128)(2,1)} %wu_hbm.1, bf16[2,5632,2048]{2,1,0:T(8,128)(2,1)} %wd_hbm.1), custom_call_target="tpu_custom_call" | custom-call | tf_op jit(solution)/shard_map/moe/pallas_call | solution.py:322
  93.8 1.1 %convert_element_type.3 = bf16[256,2048]{1,0:T(8,128)(2,1)} convert(f32[256,2048]{1,0:T(8,128)S(1)} %moe.1) | non-fusion elementwise | flops 524288 | bytes 3145728 | tf_op jit(solution)/shard_map/convert_element_type | solution.py:344

commit v9 on v8

--- a/solution.py
+++ b/solution.py
@@ -294,11 +294,10 @@
 
     for k in range(N_COLS):
         y_copy(1, 1, 1, k, partner).wait_recv()
-        if k == N_COLS - 1:
-            for peer in (2, 3):
-                y_copy(1, peer, 0, k, me).wait_recv()
-            fold(3, 3, (RECV + 4, RECV + 5), k)
         fold(0, 0, (0, RECV + 3), k)
+    for peer in (2, 3):
+        y_copy(1, peer, 0, N_COLS - 1, me).wait_recv()
+    fold(3, 3, (RECV + 4, RECV + 5), N_COLS - 1)
 
     for c in x_copies + m_copies + [p_copy]:
         c.wait_send()

time: 95 us -> 94.9 us (level)
  no operation moved by 1% of the time
where the time goes in v9:
time: 94.9 us; the launch traced here: 94.8 us
  Pallas kernels  93.6 us (99%)
  other arithmetic  1.12 us (1%)
    pallas_call x1, Pallas kernels, local_step(): pl.pallas_call(kernel, name='moe', out_shape=pltpu.VMEM((tok_n, dim), F32...  93.6 us

profile of v9, /device:TPU:0, one launch (start us, length us, event | category | flops | bytes accessed | tf_op | source)
XLA Modules:
  0.0 94.8 jit_solution(12827296213632159008)
XLA Ops:
  0.0 93.6 %moe.1 = f32[256,2048]{1,0:T(8,128)S(1)} custom-call(bf16[2,128,2048]{2,1,0:T(8,128)(2,1)} %bitcast.3, s32[2,256]{1,0:T(2,128)} %bitcast.4, f32[2,256]{1,0:T(2,128)} %bitcast.5, s32[1,8]{1,0:T(1,128)} %cnt_ref.1, bf16[2,2048,5632]{2,1,0:T(8,128)(2,1)} %wg_hbm.1, bf16[2,2048,5632]{2,1,0:T(8,128)(2,1)} %wu_hbm.1, bf16[2,5632,2048]{2,1,0:T(8,128)(2,1)} %wd_hbm.1), custom_call_target="tpu_custom_call" | custom-call | tf_op jit(solution)/shard_map/moe/pallas_call | solution.py:321
  93.6 1.1 %convert_element_type.3 = bf16[256,2048]{1,0:T(8,128)(2,1)} convert(f32[256,2048]{1,0:T(8,128)S(1)} %moe.1) | non-fusion elementwise | flops 524288 | bytes 3145728 | tf_op jit(solution)/shard_map/convert_element_type | solution.py:343
